TPU v7x, 32 devices: a whole 2x2x4 slice. The times are simulated.
32 devices in a mesh: kpt: 2 (over x), row: 8 (over z, y), col: 2 (over core).
Axes of the slice: x: 2, y: 2, z: 4, core: 2. Of those that a mesh axis runs over, the one named last changes fastest.
Arguments:
- wannier: float32 [64, 32, 1024], P('kpt', ('row', 'col')), parts along dimension 0, may hold values from -6 to 6
- pairs: int32 [384, 2], replicated, may hold values from 0 to 31, as said below
- gmap: int32 [8192], replicated, may hold values from 1 to 32767, as said below
- screened: bfloat16 [4, 2, 8192, 8192], P('kpt', None, 'row', 'col'), parts along dimension 0, may hold values from -0.046875 to 0.046875
Outputs:
- coulomb: float32 [2, 2, 768, 384], P(None, None, ('kpt', 'row', 'col')), parts along dimension 2
There are 2 independent parts, one for each index of `kpt`. A program takes and returns all parts, laid end to end along the dimension named above; an argument that names none is the same for every part. Nothing has to cross between parts.
Inputs may be any that keep to these rules, and one draw needn't show every extreme that they name: `gmap`: 8192 distinct flat cells of the grid; cell 0 is never among them. `pairs`: in each row the first Wannier function is no greater than the second; no two rows are equal.
All inputs are finite; a program needn't handle non-finite values.
Results may differ from a plain program's by a relative error of at most 0.0082.
Values may be sent and summed in bfloat16 or wider, within the bound.
No kernel may reach another device: no remote copies, remote signals or barrier semaphores. Data moves between devices by JAX's collectives and lax.ppermute only.
A program may use at most 128 MiB of HBM per device.

v0:
```python
import math

import jax
import jax.numpy as jnp
from jax import lax
from jax.sharding import PartitionSpec as P

NW = 32
GX = 32
NG = 8192
NP = 384


def line_tables(side_len):
    positions = jnp.arange(side_len, dtype=jnp.int32)
    phase_index = positions[:, None] * positions[None, :] % side_len
    angles = phase_index.astype(jnp.float32) * (2.0 * math.pi / side_len)
    return (jnp.cos(angles), jnp.sin(angles))


def plane_transform(density):
    cosine, sine_table = line_tables(GX)
    highest = lax.Precision.HIGHEST
    shaped = density.reshape(-1, GX, GX)
    real_z = jnp.einsum("nyz,kz->nyk", shaped, cosine, precision=highest)
    imag_z = -jnp.einsum("nyz,kz->nyk", shaped, sine_table, precision=highest)
    new_real = jnp.einsum("jy,nyk->njk", cosine, real_z, precision=highest) + jnp.einsum(
        "jy,nyk->njk", sine_table, imag_z, precision=highest
    )
    new_imag = jnp.einsum("jy,nyk->njk", cosine, imag_z, precision=highest) - jnp.einsum(
        "jy,nyk->njk", sine_table, real_z, precision=highest
    )
    return (new_real.reshape(density.shape), new_imag.reshape(density.shape))


def line_transform(real_part, imag_part):
    cosine, sine_table = line_tables(GX)
    highest = lax.Precision.HIGHEST
    new_real = jnp.einsum("kn,pny->pky", cosine, real_part, precision=highest) + jnp.einsum(
        "kn,pny->pky", sine_table, imag_part, precision=highest
    )
    new_imag = jnp.einsum("kn,pny->pky", cosine, imag_part, precision=highest) - jnp.einsum(
        "kn,pny->pky", sine_table, real_part, precision=highest
    )
    return (new_real, new_imag)


def right_columns(screened, segment):
    w_real = screened[:, 0]
    w_imag = screened[:, 1]
    real_real = jnp.einsum("fgh,bh->fgb", w_real, segment[0], preferred_element_type=jnp.float32)
    imag_imag = jnp.einsum("fgh,bh->fgb", w_imag, segment[1], preferred_element_type=jnp.float32)
    real_imag = jnp.einsum("fgh,bh->fgb", w_real, segment[1], preferred_element_type=jnp.float32)
    imag_real = jnp.einsum("fgh,bh->fgb", w_imag, segment[0], preferred_element_type=jnp.float32)
    return jnp.stack([real_real - imag_imag, real_imag + imag_real], axis=1)


def shards(wannier, pairs, gmap, screened):
    planes = wannier.shape[1]
    grid_cells = wannier.shape[2]
    members = jnp.arange(NW, dtype=jnp.int32)[None, :]
    pick_first = (pairs[:, 0:1] == members).astype(jnp.float32)
    pick_second = (pairs[:, 1:2] == members).astype(jnp.float32)
    flat_rows = wannier.reshape(NW, -1)
    highest = lax.Precision.HIGHEST
    density = jnp.dot(pick_first, flat_rows, precision=highest) * jnp.dot(
        pick_second, flat_rows, precision=highest
    )
    density = density.reshape(NP, planes, grid_cells)
    arrived = lax.all_to_all(density, ("row", "col"), split_axis=0, concat_axis=1, tiled=True)
    real_part, imag_part = plane_transform(arrived)
    real_part, imag_part = line_transform(real_part, imag_part)
    owned = real_part.shape[0]
    norm_factor = 1.0 / math.sqrt(GX * GX * GX)
    rho_real = jnp.take(real_part.reshape(owned, -1), gmap, axis=1) * norm_factor
    rho_imag = jnp.take(imag_part.reshape(owned, -1), gmap, axis=1) * norm_factor
    rho = jnp.stack([rho_real, rho_imag], axis=0).astype(jnp.bfloat16)
    row_span = screened.shape[2]
    halves = lax.all_to_all(rho, "col", split_axis=2, concat_axis=1, tiled=True)
    screened_rho = right_columns(screened, lax.all_gather(halves, "row", axis=1, tiled=True))
    blocks = lax.all_to_all(rho, "row", split_axis=2, concat_axis=1, tiled=True)
    blocks = blocks.reshape(2, lax.axis_size("row"), owned, row_span)
    left_panel = lax.all_gather(blocks, "col", axis=2, tiled=True).reshape(2, NP, row_span)
    left_wide = left_panel.astype(jnp.float32)
    u_real = jnp.einsum(
        "ag,fgb->fab", left_wide[0], screened_rho[:, 0], precision=highest
    ) + jnp.einsum("ag,fgb->fab", left_wide[1], screened_rho[:, 1], precision=highest)
    u_imag = jnp.einsum(
        "ag,fgb->fab", left_wide[0], screened_rho[:, 1], precision=highest
    ) - jnp.einsum("ag,fgb->fab", left_wide[1], screened_rho[:, 0], precision=highest)
    partial_terms = jnp.stack([u_real, u_imag], axis=1) / math.sqrt(NG)
    summed = lax.psum(partial_terms, ("row", "col"))
    share_rows = NP // lax.axis_size(("row", "col"))
    return lax.dynamic_slice_in_dim(
        summed, lax.axis_index(("row", "col")) * share_rows, share_rows, 2
    )


def solution(mesh):
    return jax.shard_map(
        shards,
        mesh=mesh,
        in_specs=(P("kpt", ("row", "col"), None), P(), P(), P("kpt", None, "row", "col")),
        out_specs=P(None, None, ("kpt", "row", "col"), None),
        check_vma=False,
    )
```

profile of v0, /device:TPU:0, one launch (start us, length us, event | category | flops | bytes accessed | tf_op | source)
XLA Modules:
  0.0 687.3 jit_solution(8600309741713015094)
XLA Ops:
  11.3 3.8 reshape.35
  15.1 7.5 %all-to-all-start = ((f32[384,2,1024]{2,1,0:T(2,128)}), f32[384,2,1024]{2,1,0:T(2,128)S(1)}, u32[]{:S(2)}, u32[]{:S(2)}) async-start(f32[384,2,1024]{2,1,0:T(2,128)} %reshape.35), calls=%async_computation | async-start | bytes 6291456 | tf_op jit(solution)/shard_map/all_to_all | solution.py:70
  22.7 59.1 %all-to-all-done = f32[384,2,1024]{2,1,0:T(2,128)S(1)} async-done(((f32[384,2,1024]{2,1,0:T(2,128)}), f32[384,2,1024]{2,1,0:T(2,128)S(1)}, u32[]{:S(2)}, u32[]{:S(2)}) %all-to-all-start) | async-done | bytes 3145760 | tf_op jit(solution)/shard_map/all_to_all | solution.py:70
  82.9 2.4 copy.71
  85.3 7.6 %reshape.36 = f32[768,32,32]{2,1,0:T(8,128)} reshape(f32[24,16,2,1024]{3,2,1,0:T(2,128)S(1)} %copy.71) | data formatting | bytes 6291456 | tf_op jit(solution)/shard_map/reshape | solution.py:24
  92.9 9.2 %copy.72 = f32[768,32,32]{0,2,1:T(8,128)S(1)} copy(f32[768,32,32]{2,1,0:T(8,128)} %reshape.36) | data formatting | bytes 6291456 | tf_op jit(solution)/shard_map/reshape | solution.py:24
  102.1 3.0 convolution_negate_fusion
  105.1 3.0 fusion.72
  108.1 4.9 fusion.22
  113.1 5.2 fusion.24
  118.2 6.7 add_bitcast_fusion.1
  125.0 5.5 subtract_bitcast_fusion.1
  130.5 10.6 %copy.79 = f32[768,32,32]{2,1,0:T(8,128)} copy(f32[768,32,32]{0,1,2:T(8,128)S(1)} %subtract_bitcast_fusion.1) | data formatting | bytes 6291456 | tf_op jit(solution)/shard_map/sub | solution.py:30
  141.1 9.4 %reshape.38 = f32[24,32,1024]{2,1,0:T(8,128)S(1)} reshape(f32[768,32,32]{2,1,0:T(8,128)} %copy.79) | data formatting | bytes 6291456 | tf_op jit(solution)/shard_map/reshape | solution.py:33
  150.4 5.5 fusion.66
  155.9 11.4 %copy.76 = f32[768,32,32]{2,1,0:T(8,128)} copy(f32[768,32,32]{0,1,2:T(8,128)} %add_bitcast_fusion.1) | data formatting | bytes 6291456 | tf_op jit(solution)/shard_map/add | solution.py:27
  167.3 10.7 %reshape.37 = f32[24,32,1024]{2,1,0:T(8,128)} reshape(f32[768,32,32]{2,1,0:T(8,128)} %copy.76) | data formatting | bytes 6291456 | tf_op jit(solution)/shard_map/reshape | solution.py:33
  178.0 5.9 fusion.69
  184.0 5.5 subtract_bitcast_fusion
  189.5 5.6 add_bitcast_fusion
  195.1 10.3 %copy.89 = f32[24,32,1024]{0,2,1:T(8,128)} copy(f32[24,32,1024]{2,1,0:T(8,128)} %add_bitcast_fusion) | data formatting | bytes 6291456 | tf_op jit(solution)/shard_map/reshape | solution.py:75
  205.4 8.6 %copy.90 = f32[24,32,1024]{0,2,1:T(8,128)} copy(f32[24,32,1024]{2,1,0:T(8,128)S(1)} %copy-done.2) | data formatting | bytes 6291456 | tf_op jit(solution)/shard_map/reshape | solution.py:76
  214.0 33.6 %gather_fusion = f32[8192,24]{1,0:T(8,128)} fusion(f32[24,32768]{0,1:T(8,128)} %bitcast.144, s32[8192]{0:T(1024)S(1)} %fusion.57), kind=kCustom, calls=%fused_computation.clone | custom fusion | bytes 1605632 | tf_op jit(solution)/shard_map/jit(_take)/gather | solution.py:75
  247.6 33.6 %gather_fusion.1 = f32[8192,24]{1,0:T(8,128)} fusion(f32[24,32768]{0,1:T(8,128)} %bitcast.143, s32[8192]{0:T(1024)S(1)} %fusion.57), kind=kCustom, calls=%fused_computation.1.clone | custom fusion | bytes 1605632 | tf_op jit(solution)/shard_map/jit(_take)/gather | solution.py:76
  281.3 7.2 %fusion.30 = (bf16[1,24,8192]{1,2,0:T(8,128)(2,1)S(1)}, bf16[1,24,8192]{1,2,0:T(8,128)(2,1)S(1)}) fusion(f32[8192,24]{1,0:T(8,128)} %gather_fusion, pred[8192]{0:T(1024)(128)(4,1)S(1)} %compare_and_fusion, f32[8192,24]{1,0:T(8,128)} %gather_fusion.1), kind=kLoop, calls=%fused_computation.43 | loop fusion | flops 1179648 | bytes 2367488 | tf_op jit(solution)/shard_map/stack | solution.py:77
  289.4 35.5 %copy.108 = bf16[2,24,8192]{1,0,2:T(2,128)(2,1)} copy(bf16[2,24,8192]{1,2,0:T(8,128)(2,1)S(1)} %pad_maximum_fusion) | data formatting | bytes 1572864 | tf_op jit(solution)/shard_map/stack | solution.py:77
  324.9 6.6 reshape.71
  331.5 35.8 %all_to_all.48 = bf16[8,2,24576]{2,1,0:T(2,128)(2,1)S(1)} all-to-all(bf16[8,2,24576]{2,1,0:T(2,128)(2,1)S(1)} %reshape.71), channel_id=1, replica_groups=mesh['kpt'=2,'row'=8,'col'=2] {'row'}, dimensions={0} | all-to-all | bytes 1572864 | tf_op jit(solution)/shard_map/all_to_all | solution.py:81
  367.3 6.9 %reshape.72 = bf16[8192,2,24]{2,1,0:T(2,128)(2,1)} reshape(bf16[8,2,24576]{2,1,0:T(2,128)(2,1)S(1)} %all_to_all.48) | data formatting | bytes 1572864
  374.3 10.3 %copy.87 = bf16[2,24,8,1024]{3,1,2,0:T(8,128)(2,1)} copy(bf16[2,24,8,1024]{1,0,3,2:T(2,128)(2,1)} %bitcast.145) | data formatting | bytes 1572864 | tf_op jit(solution)/shard_map/all_to_all | solution.py:81
  384.6 10.2 %copy.109 = bf16[2,24,8192]{1,0,2:T(2,128)(2,1)} copy(bf16[2,24,8192]{1,2,0:T(8,128)(2,1)} %copy-done) | data formatting | bytes 1572864 | tf_op jit(solution)/shard_map/stack | solution.py:77
  394.8 7.0 %reshape.73 = bf16[2,2,98304]{2,1,0:T(2,128)(2,1)S(1)} reshape(bf16[8192,2,24]{2,1,0:T(2,128)(2,1)} %bitcast.147) | data formatting | bytes 1572864
  401.9 4.4 all_to_all.49
  406.2 7.3 %reshape.74 = bf16[8192,2,24]{2,1,0:T(2,128)(2,1)} reshape(bf16[2,2,98304]{2,1,0:T(2,128)(2,1)S(1)} %all_to_all.49) | data formatting | bytes 1572864
  413.6 9.5 %copy.83 = bf16[2,24,2,4096]{3,1,2,0:T(8,128)(2,1)} copy(bf16[2,24,2,4096]{1,0,3,2:T(2,128)(2,1)} %bitcast.146) | data formatting | bytes 1572864 | tf_op jit(solution)/shard_map/all_to_all | solution.py:79
  423.1 1.5 fusion.129
  424.7 96.3 %all-gather.3.cloned.1.call-done = bf16[2,384,4096]{2,1,0:T(8,128)(2,1)} async-done(((bf16[2,48,4096]{2,1,0:T(8,128)(2,1)}), bf16[2,384,4096]{2,1,0:T(8,128)(2,1)}) %all-gather.3.cloned.1.call-update) | async-done | bytes 6291472 | tf_op jit(solution)/shard_map/all_gather | solution.py:80
  521.0 11.4 %fusion = f32[384,2,1024]{2,0,1:T(8,128)S(1)} fusion(bf16[2,2,1024,4096]{3,2,1,0:T(8,128)(2,1)} %param.9, bf16[2,384,4096]{2,1,0:T(8,128)(2,1)} %all-gather.3.cloned.1.call-done), kind=kOutput, calls=%fused_computation.2 | convolution fusion | flops 6442450944 | bytes 23068672 | tf_op jit(solution)/shard_map/fgh,bh->fgb/dot_general | solution.py:54
  532.4 11.2 %fusion.39 = f32[384,2,1024]{2,0,1:T(8,128)S(1)} fusion(f32[384,2,1024]{2,0,1:T(8,128)S(1)} %fusion, bf16[2,2,1024,4096]{3,2,1,0:T(8,128)(2,1)} %param.9, bf16[2,384,4096]{2,1,0:T(8,128)(2,1)} %all-gather.3.cloned.1.call-done), kind=kOutput, calls=%fused_computation.47 | convolution fusion | flops 6443237376 | bytes 26214400 | tf_op jit(solution)/shard_map/fgh,bh->fgb/dot_general | solution.py:53
  543.6 2.6 fusion.14
  546.2 2.6 fusion.16
  548.9 12.6 %fusion.2 = f32[384,2,1024]{2,0,1:T(8,128)} fusion(bf16[2,2,1024,4096]{3,2,1,0:T(8,128)(2,1)} %param.9, bf16[2,384,4096]{2,1,0:T(8,128)(2,1)} %all-gather.3.cloned.1.call-done), kind=kOutput, calls=%fused_computation.4 | convolution fusion | flops 6442450944 | bytes 23068672 | tf_op jit(solution)/shard_map/fgh,bh->fgb/dot_general | solution.py:52
  561.5 12.1 %fusion.36 = f32[384,2,1024]{2,0,1:T(8,128)S(1)} fusion(f32[384,2,1024]{2,0,1:T(8,128)} %fusion.2, bf16[2,2,1024,4096]{3,2,1,0:T(8,128)(2,1)} %param.9, bf16[2,384,4096]{2,1,0:T(8,128)(2,1)} %all-gather.3.cloned.1.call-done), kind=kOutput, calls=%fused_computation.46 | convolution fusion | flops 6443237376 | bytes 26214400 | tf_op jit(solution)/shard_map/fgh,bh->fgb/dot_general | solution.py:51
  573.6 2.7 fusion.48
  576.3 2.7 fusion.51
  579.0 1.6 maximum_multiply_fusion
  580.6 97.4 %all-reduce.2.cloned.1.call-done = f32[2,2,384,384]{2,3,0,1:T(8,128)} async-done(((f32[2,2,384,384]{2,3,0,1:T(8,128)}), f32[2,2,384,384]{2,3,0,1:T(8,128)}) %all-reduce.2.cloned.1.call-update) | async-done | bytes 2359312 | tf_op jit(solution)/shard_map/psum | solution.py:92
  678.0 1.7 constant_dynamic-slice_fusion
  (26 shorter events, 7.9 us)
Async XLA Ops:
  15.1 7.6 %copy-start.4 = (s32[8192]{0:T(1024)S(1)}, s32[8192]{0:T(1024)}, u32[]{:S(2)}) copy-start(s32[8192]{0:T(1024)} %param.8) | copy-start | bytes 98308
  15.1 66.8 %all-to-all-start = ((f32[384,2,1024]{2,1,0:T(2,128)}), f32[384,2,1024]{2,1,0:T(2,128)S(1)}, u32[]{:S(2)}, u32[]{:S(2)}) async-start(f32[384,2,1024]{2,1,0:T(2,128)} %reshape.35), calls=%async_computation | async-start | bytes 6291456 | tf_op jit(solution)/shard_map/all_to_all | solution.py:70
  22.6 400.5 %all-gather.5.cloned.1.call-start = ((), (), s32[]{:S(2)}) async-start(), calls=%async_computation.4 | async-start | bytes 2359296 | tf_op jit(solution)/shard_map/all_gather | solution.py:83
  178.0 6.0 copy-start.1
  178.0 6.0 copy-start.3
  195.1 10.3 %copy-start.2 = (f32[24,32,1024]{2,1,0:T(8,128)S(1)}, f32[24,32,1024]{2,1,0:T(8,128)}, u32[]{:S(2)}) copy-start(f32[24,32,1024]{2,1,0:T(8,128)} %subtract_bitcast_fusion) | copy-start | bytes 9437188
  289.4 35.5 %copy-start = (bf16[2,24,8192]{1,2,0:T(8,128)(2,1)}, bf16[2,24,8192]{1,2,0:T(8,128)(2,1)S(1)}, u32[]{:S(2)}) copy-start(bf16[2,24,8192]{1,2,0:T(8,128)(2,1)S(1)} %pad_maximum_fusion) | copy-start | bytes 2359300
  384.6 136.4 %all-gather.3.cloned.1.call-start = ((), (), s32[]{:S(2)}) async-start(), calls=%async_computation.3 | async-start | bytes 7077888 | tf_op jit(solution)/shard_map/all_gather | solution.py:80
  423.1 254.9 %all-reduce.2.cloned.1.call-start = ((), (), s32[]{:S(2)}) async-start(), calls=%async_computation.5 | async-start | bytes 4718592 | tf_op jit(solution)/shard_map/psum | solution.py:92
Sparse Core Ops, SparseCore 0:
  384.7 8.8 all-gather.4
  423.2 97.7 all-gather.2
  580.7 97.1 all-reduce.1
where the time goes:
time: 696 us; the launch traced here: 687 us
  waiting for transfers between devices  253 us (36%)
  local copies, waits for them, and re-layouts  251 us (36%)
  matrix products  112 us (16%)
  blocking collectives  40.1 us (6%)
  between operations  13.7 us (2%)
  other arithmetic  9.75 us (1%)
  starting transfers between devices  7.67 us (1%)
    psum x1, waiting for transfers between devices, shards(): summed = lax.psum(partial_terms, ('row', 'col'))  97.4 us
    all_gather x1, waiting for transfers between devices, shards(): lax.all_gather(halves, 'row', axis=1, tiled=True)  96.3 us
    all_to_all x1, waiting for transfers between devices, shards(): lax.all_to_all(density, ('row', 'col'), split_axis=0, concat_axis=1, tile...  59.1 us
    another operation x2, local copies, waits for them, and re-layouts, shards(): rho = jnp.stack([rho_real, rho_imag], axis=0).astype(jnp.bfloat16)  45.7 us
    all_to_all x1, blocking collectives, shards(): blocks = lax.all_to_all(rho, 'row', split_axis=2, concat_axis=1, tiled=True)  35.8 us
    gather x1, local copies, waits for them, and re-layouts, shards(): jnp.take(imag_part.reshape(owned, -1), gmap, axis=1) * norm_factor  33.6 us
    gather x1, local copies, waits for them, and re-layouts, shards(): jnp.take(real_part.reshape(owned, -1), gmap, axis=1) * norm_factor  33.6 us
    unnamed x15, local copies, waits for them, and re-layouts  29 us
  transfers between devices with their start and end apart: 4, of which 3 were waited for; matrix products, arithmetic and copies ran while one was open for 5% of the time, Pallas kernels for 0%

commit v1 on v0

v1 whole, which is shorter than its diff:
```python
import functools
import math

import jax
import jax.numpy as jnp
import numpy as np
from jax import lax
from jax.experimental import pallas as pl
from jax.experimental.pallas import tpu as pltpu
from jax.sharding import PartitionSpec as P

BF = jnp.bfloat16
F32 = jnp.float32
SCALE = 1.62455
VMEM_BYTES = 67_043_328


def stage_tables(side):
    half = side // 2 + 1
    positions = np.arange(side)
    angles = 2.0 * np.pi * (np.outer(positions, positions) % side) / side
    cosine, sine = SCALE * np.cos(angles), SCALE * np.sin(angles)
    z_table = np.zeros((half, 2, 8, 8, side))
    for y in range(8):
        z_table[:, 0, y, y, :] = cosine[:half]
        z_table[:, 1, y, y, :] = -sine[:half]
    line = np.zeros((side, 2, side, 2))
    line[:, 0, :, 0] = cosine
    line[:, 0, :, 1] = sine
    line[:, 1, :, 0] = -sine
    line[:, 1, :, 1] = cosine
    y_one = line.reshape(side // 4, 4, 2, side // 8, 8, 2).transpose(0, 2, 1, 3, 5, 4)
    y_one = y_one.reshape(2 * side, 2 * side)
    x_four = np.einsum("koni,ab->okanib", line, np.eye(4)).reshape(8 * side, 8 * side)
    z_table = z_table.reshape(16 * half, 8 * side)
    tables = (z_table, np.kron(np.eye(4), y_one), y_one, x_four)
    return [jnp.asarray(table.astype(np.float32)).astype(BF) for table in tables]


def dot_nt(a, b):
    return lax.dot_general(a, b, (((1,), (1,)), ((), ())), preferred_element_type=F32)


def dot_nn(a, b):
    return lax.dot_general(a, b, (((1,), (0,)), ((), ())), preferred_element_type=F32)


def dot_tn(a, b):
    return lax.dot_general(a, b, (((0,), (0,)), ((), ())), preferred_element_type=F32)


def log2(n):
    return n.bit_length() - 1


def pair_kernel(side, planes, rows, norm, info, cells, signs, *refs):
    pieces = refs[: 2 * rows]
    picks, zt, yt, ys, xt, send, keep, wann, mid1, mid2, spec, stage, sems = refs[2 * rows :]
    half = side // 2 + 1
    me_row, me_col = info[0], info[1]
    lanes = mid2.shape[-1]
    own = lanes * 3 // 4

    copies = [
        pltpu.make_async_copy(piece, wann.at[pl.ds(index * planes, planes)], sems.at[index])
        for index, piece in enumerate(pieces)
    ]
    for copy in copies:
        copy.start()
    for copy in copies:
        copy.wait()

    def plane_pair(xp, carry):
        for h in range(2):
            x = 2 * xp + h
            from_row = lax.shift_right_logical(x, log2(2 * planes))
            from_col = lax.shift_right_logical(x, log2(planes)) & 1
            place = ((from_col ^ me_col) * rows + (from_row ^ me_row)) * planes
            plane = wann[place + (x & (planes - 1))]
            high = plane.astype(BF)
            low = (plane - high.astype(F32)).astype(BF)
            both = dot_nn(picks[...], jnp.concatenate([high, low], axis=0))
            density = (both[:own] * both[own:]).astype(BF)
            density = jnp.concatenate([density, density[lanes // 2 : own]], axis=0)
            for t in range(side // 8):
                lines = dot_nt(zt[...], density[:, t * 8 * side : (t + 1) * 8 * side])
                mid1[h, :, t] = lines.astype(BF).reshape(half, 16, lanes)
        for q in range(half // 4 + 1):
            parts = []
            for h in range(2):
                if q < half // 4:
                    lines = mid1[h, 4 * q : 4 * q + 4].reshape(8 * side, lanes)
                    parts.append(dot_nn(yt[...], lines))
                else:
                    parts.append(dot_nn(ys[...], mid1[h, half - 1].reshape(2 * side, lanes)))
            groups = parts[0].shape[0] // 8
            joined = jnp.concatenate([p.reshape(groups, 8, lanes) for p in parts], axis=1)
            mid2[pl.ds(q * side, groups), xp] = joined.astype(BF)
        return carry

    lax.fori_loop(0, side // 2, plane_pair, 0)

    left = lax.broadcasted_iota(jnp.int32, (1, 128), 1) < 64

    def column(kq, carry):
        lines = dot_nn(xt[...], mid2[kq].reshape(8 * side, lanes))
        n = 4 * side
        re, im = lines[:n], lines[n:]
        last = jnp.where(left, re[:, 128:], im[:, 128:])
        spec[pl.ds(kq * n, n), 0, :] = jnp.concatenate([re[:, :128], im[:, :128], last], axis=1)
        return carry

    lax.fori_loop(0, mid2.shape[0], column, 0, unroll=2)

    block = stage.shape[0]
    lane = lax.broadcasted_iota(jnp.int32, (1, 384), 1)
    imag = ((lane >= 128) & (lane < 256)) | (lane >= 320)

    def gather_into(out, first):
        def step(b, carry):
            base = first + b * block
            for j in range(block):
                row = spec[cells[base + j]]
                stage[j] = row * jnp.where(imag, signs[base + j], norm)
            out[pl.ds(pl.multiple_of(b * block, block), block), :] = stage[:, 0, :].astype(BF)
            return carry

        lax.fori_loop(0, out.shape[0] // block, step, 0)

    gather_into(send, 0)
    gather_into(keep, send.shape[0])


def pair_coefficients(info, cells, signs, pieces, picks, side, norm, send_rows):
    keep_rows = cells.shape[0] - send_rows
    planes, members = pieces[0].shape[:2]
    half = side // 2 + 1
    lanes = 256
    smem = pl.BlockSpec(memory_space=pltpu.SMEM)
    vmem = pl.BlockSpec(memory_space=pltpu.VMEM)
    return pl.pallas_call(
        functools.partial(pair_kernel, side, planes, len(pieces) // 2, norm),
        out_shape=(
            jax.ShapeDtypeStruct((send_rows, 384), BF),
            jax.ShapeDtypeStruct((keep_rows, 384), BF),
        ),
        in_specs=[smem] * 3 + [pl.BlockSpec(memory_space=pl.ANY)] * len(pieces) + [vmem] * 5,
        out_specs=(vmem, vmem),
        scratch_shapes=[
            pltpu.VMEM((side, members, side * side), F32),
            pltpu.VMEM((2, half, side // 8, 16, lanes), BF),
            pltpu.VMEM((half * side // 4, side // 2, 16, lanes), BF),
            pltpu.VMEM((half * side * side, 1, 384), F32),
            pltpu.VMEM((32, 1, 384), F32),
            pltpu.SemaphoreType.DMA((len(pieces),)),
        ],
        compiler_params=pltpu.CompilerParams(vmem_limit_bytes=VMEM_BYTES),
        cost_estimate=pl.CostEstimate(
            flops=30_000_000_000, bytes_accessed=12_000_000, transcendentals=0
        ),
        name="pair_coefficients",
    )(info, cells, signs, *pieces, picks, *stage_tables(side))


def ordered(mine, theirs, is_first):
    first = jnp.where(is_first, mine, theirs)
    second = jnp.where(is_first, theirs, mine)
    left = lax.broadcasted_iota(jnp.int32, (1, 128), 1) < 64
    a, b = first[:, 256:], second[:, 256:]
    re = jnp.concatenate(
        [first[:, :128], second[:, :128], jnp.where(left, a, pltpu.roll(b, 64, 1))], axis=1
    )
    im = jnp.concatenate(
        [first[:, 128:256], second[:, 128:256], jnp.where(left, pltpu.roll(a, 64, 1), b)], axis=1
    )
    return re, im


def coulomb_kernel(
    steps, shares, scale, info, keep, send_g, recv, recv_g, w, mine, other, r0, r1, lhs, mixed
):
    step = pl.program_id(1)
    is_first = info[1] == 0
    pairs = r0.shape[1] // 2

    @pl.when((pl.program_id(0) == 0) & (step == 0))
    def _():
        chunk = 256

        def build(i, carry):
            at = pl.ds(pl.multiple_of(i * chunk, chunk), chunk)
            re, im = ordered(keep[at, :].astype(F32), recv[at, :].astype(F32), is_first)
            r0[at, :] = jnp.concatenate([re, im], axis=1).astype(BF)
            r1[at, :] = jnp.concatenate([-im, re], axis=1).astype(BF)
            return carry

        lax.fori_loop(0, keep.shape[0] // chunk, build, 0)

        def build_left(i, carry):
            at = pl.ds(pl.multiple_of(i * chunk, chunk), chunk)
            re, im = ordered(send_g[at, :].astype(F32), recv_g[at, :].astype(F32), is_first)
            lhs[at, :] = jnp.concatenate([re, im], axis=1).astype(BF)
            return carry

        lax.fori_loop(0, lhs.shape[0] // chunk, build_left, 0)

    tile = w.shape[2]
    product = dot_nn(w[0, 0], r0[...]) + dot_nn(w[0, 1], r1[...])
    mixed[pl.ds(pl.multiple_of(step * tile, tile), tile), :] = product.astype(BF)

    @pl.when(step == steps - 1)
    def _():
        re_rows = dot_tn(lhs[:, :pairs], mixed[...])
        im_rows = dot_tn(lhs[:, pairs:], mixed[...])
        u = (
            (re_rows[:, :pairs] + im_rows[:, pairs:]) * scale,
            (re_rows[:, pairs:] - im_rows[:, :pairs]) * scale,
        )
        n = pairs // shares

        def put(even, odd):
            for part in range(2):
                for s in range(shares):
                    target = odd if s % 2 else even
                    target[s // 2, 0, part] = u[part][s * n : (s + 1) * n]

        @pl.when(is_first)
        def _():
            put(mine, other)

        @pl.when(jnp.logical_not(is_first))
        def _():
            put(other, mine)


def coulomb_partial(info, keep, send, recv, screened, rows, scale):
    freqs, _, g_rows, h_rows = screened.shape
    pairs = keep.shape[1]
    tile = min(256, g_rows)
    steps = g_rows // tile
    shares = 2 * rows
    shape = (rows, freqs, 2, pairs // shares, pairs)
    once = pl.Buffered(1)

    def fixed(n, index):
        return pl.BlockSpec((n, pairs), lambda f, i: (index, 0), pipeline_mode=once)

    out_spec = pl.BlockSpec((rows, 1) + shape[2:], lambda f, i: (0, f, 0, 0, 0))
    return pl.pallas_call(
        functools.partial(coulomb_kernel, steps, shares, scale),
        grid=(freqs, steps),
        out_shape=(jax.ShapeDtypeStruct(shape, F32),) * 2,
        in_specs=[
            pl.BlockSpec(memory_space=pltpu.SMEM),
            fixed(h_rows, 0),
            fixed(g_rows, h_rows // g_rows),
            fixed(h_rows, 0),
            fixed(g_rows, h_rows // g_rows),
            pl.BlockSpec((1, 2, tile, h_rows), lambda f, i: (f, 0, i, 0)),
        ],
        out_specs=(out_spec, out_spec),
        scratch_shapes=[
            pltpu.VMEM((h_rows, 2 * pairs), BF),
            pltpu.VMEM((h_rows, 2 * pairs), BF),
            pltpu.VMEM((g_rows, 2 * pairs), BF),
            pltpu.VMEM((g_rows, 2 * pairs), BF),
        ],
        compiler_params=pltpu.CompilerParams(vmem_limit_bytes=VMEM_BYTES),
        cost_estimate=pl.CostEstimate(
            flops=28_000_000_000, bytes_accessed=45_000_000, transcendentals=0
        ),
        name="coulomb_partial",
    )(info, keep, send, recv, recv, screened)


def cell_table(gmap, side, norm):
    kx, ky, kz = gmap // (side * side), gmap // side % side, gmap % side
    mirrored = kz > side // 2
    kx, ky, kz = (jnp.where(mirrored, -k % side, k) for k in (kx, ky, kz))
    cells = ((kz * (side // 4) + ky // 4) * side + kx) * 4 + ky % 4
    return cells, jnp.where(mirrored, -norm, norm).astype(F32)


def shards(rows, cols, wannier, pairs, gmap, screened):
    members, planes, grid_cells = wannier.shape
    side = math.isqrt(grid_cells)
    count = pairs.shape[0]
    waves = gmap.shape[0]
    g_rows, h_rows = screened.shape[2:]
    row, col = lax.axis_index("row"), lax.axis_index("col")
    info = jnp.stack([row, col]).astype(jnp.int32)
    swap = [(0, 1), (1, 0)]

    local = wannier.transpose(1, 0, 2)
    same = [local]
    for shift in range(1, rows):
        same.append(lax.ppermute(local, "row", [(i, i ^ shift) for i in range(rows)]))
    cross = [lax.ppermute(piece, "col", swap) for piece in same]

    wide = count // 3
    first = lax.dynamic_slice_in_dim(pairs, col * wide, wide, 0)
    last = lax.dynamic_slice_in_dim(pairs, 2 * wide + col * (wide // 2), wide // 2, 0)
    owned = jnp.concatenate([first, last], axis=0).T.reshape(-1, 1)
    picks = (owned == jnp.arange(2 * members, dtype=jnp.int32)[None, :] % members).astype(BF)

    norm = 1.0 / (math.sqrt(side**3) * SCALE**3)
    cells, signs = cell_table(gmap, side, norm)

    def arranged(table):
        theirs = lax.dynamic_slice_in_dim(table, (1 - col) * h_rows, h_rows)
        block = lax.dynamic_slice_in_dim(table, row * g_rows, g_rows)
        ours = lax.dynamic_slice_in_dim(table, col * h_rows, h_rows)
        return jnp.concatenate([theirs, block, ours])

    send, keep = pair_coefficients(
        info, arranged(cells), arranged(signs), same + cross, picks, side, norm, h_rows + g_rows
    )
    recv = lax.ppermute(send, "col", swap)
    mine, other = coulomb_partial(
        info, keep, send, recv, screened, rows, 1.0 / math.sqrt(waves)
    )
    chip = mine + lax.ppermute(other, "col", swap)
    spread = lax.all_to_all(chip.astype(BF), "row", split_axis=0, concat_axis=0, tiled=True)
    return jnp.sum(spread.astype(F32), axis=0)


def solution(mesh):
    rows, cols = mesh.shape["row"], mesh.shape["col"]
    return jax.shard_map(
        functools.partial(shards, rows, cols),
        mesh=mesh,
        in_specs=(P("kpt", ("row", "col"), None), P(), P(), P("kpt", None, "row", "col")),
        out_specs=P(None, None, ("kpt", "row", "col"), None),
        check_vma=False,
    )
```

time: 696 us -> 215 us (0.31); the launches traced: 687 us -> 214 us
  local copies, waits for them, and re-layouts: 251 us -> 4.38 us
  waiting for transfers between devices: 253 us -> 23.3 us
  Pallas kernels: 0 us -> 120 us
  matrix products: 112 us -> 0 us
  starting transfers between devices: 7.67 us -> 39 us
  blocking collectives: 40.1 us -> 21.2 us
  between operations: 13.7 us -> 0.19 us
    pallas_call x0 -> x2, Pallas kernels: none -> 120 us  [the longest x1 80.7 us: pair_coefficients(): pl.pallas_call(functools.partial(pair_kernel, side, planes, len(pieces) /...]
    dot_general x20 -> x0, matrix products: 112 us -> none  [the longest x1 12.6 us: right_columns(): jnp.einsum('fgh,bh->fgb', w_imag, segment[1], preferred_element_type=jnp....]
    psum x1 -> x0, waiting for transfers between devices: 97.4 us -> none  [shards(): summed = lax.psum(partial_terms, ('row', 'col'))]
    all_gather x2 -> x0, waiting for transfers between devices: 96.3 us -> none  [the longest x1 96.3 us: shards(): lax.all_gather(halves, 'row', axis=1, tiled=True)]
    gather x2 -> x0, local copies, waits for them, and re-layouts: 67.3 us -> none  [the longest x1 33.6 us: shards(): jnp.take(imag_part.reshape(owned, -1), gmap, axis=1) * norm_factor]
    reshape x7 -> x0, local copies, waits for them, and re-layouts: 59.4 us -> none  [the longest x2 20 us: plane_transform(): return (new_real.reshape(density.shape), new_imag.reshape(density.shape))]
    all_to_all x1 -> x0, waiting for transfers between devices: 59.1 us -> none  [shards(): lax.all_to_all(density, ('row', 'col'), split_axis=0, concat_axis=1, tile...]
    another operation x2 -> x0, local copies, waits for them, and re-layouts: 45.7 us -> none  [shards(): rho = jnp.stack([rho_real, rho_imag], axis=0).astype(jnp.bfloat16)]
  transfers between devices with their start and end apart: 4 -> 17, of which waited for: 3 -> 5; matrix products, arithmetic and copies ran while one was open for 5% -> 3% of each run, Pallas kernels for 0% -> 0%
where the time goes in v1:
time: 215 us; the launch traced here: 214 us
  Pallas kernels  120 us (56%)
  starting transfers between devices  39 us (18%)
  waiting for transfers between devices  23.3 us (11%)
  blocking collectives  21.2 us (10%)
  other arithmetic  6.56 us (3%)
  local copies, waits for them, and re-layouts  4.38 us (2%)
    pallas_call x1, Pallas kernels, pair_coefficients(): pl.pallas_call(functools.partial(pair_kernel, side, planes, len(pieces) /...  80.7 us
    pallas_call x1, Pallas kernels, coulomb_partial(): pl.pallas_call(functools.partial(coulomb_kernel, steps, shares, scale), g...  39.1 us
    ppermute x7, starting transfers between devices, shards(): lax.ppermute(local, 'row', [(i, i ^ shift) for i in range(rows)])  36.1 us
    all_to_all x1, blocking collectives, shards(): lax.all_to_all(chip.astype(BF), 'row', split_axis=0, concat_axis=0, tiled...  21.2 us
    ppermute x7, waiting for transfers between devices, shards(): lax.ppermute(local, 'row', [(i, i ^ shift) for i in range(rows)])  13.8 us
    ppermute x1, waiting for transfers between devices, shards(): recv = lax.ppermute(send, 'col', swap)  6.75 us
  transfers between devices with their start and end apart: 17, of which 5 were waited for; matrix products, arithmetic and copies ran while one was open for 3% of the time, Pallas kernels for 0%

profile of v1, /device:TPU:0, one launch (start us, length us, event | category | flops | bytes accessed | tf_op | source)
XLA Modules:
  0.0 214.3 jit_solution(1450362822768793934)
XLA Ops:
  0.0 1.0 copy.11
  1.0 0.6 collective-permute-start.7
  1.6 5.6 %collective-permute-start.6 = (f32[2,32,1024]{2,1,0:T(8,128)S(1)}, f32[2,32,1024]{2,1,0:T(8,128)S(1)}, u32[]{:S(2)}, u32[]{:S(2)}) collective-permute-start(f32[2,32,1024]{2,1,0:T(8,128)S(1)} %bitcast.8), channel_id=1, source_target_pairs={{0,14},{2,12},{4,10},{6,8},{8,6},{10,4},{12,2},{14,0},{1,15},{3,13... | collective-permute-start | bytes 786440 | tf_op jit(solution)/shard_map/ppermute | solution.py:297
  7.2 0.2 collective-permute-start.5
  7.4 0.7 collective-permute-start.4
  8.2 2.0 collective-permute-start.3
  10.2 0.9 fusion.9
  11.1 0.8 compare_select_fusion
  11.9 0.8 constant_dynamic-slice_fusion
  12.7 0.7 constant_dynamic-slice_fusion.1
  13.4 0.6 pad_add_fusion.cells
  14.0 0.0 collective-permute-done.7.refs_8_
  14.0 2.3 %collective-permute-start.2 = (f32[2,32,1024]{2,1,0:T(8,128)S(1)}, f32[2,32,1024]{2,1,0:T(8,128)S(1)}, u32[]{:S(2)}, u32[]{:S(2)}) collective-permute-start(f32[2,32,1024]{2,1,0:T(8,128)S(1)} %bitcast.12), channel_id=1, source_target_pairs={{0,6},{2,4},{4,2},{6,0},{8,14},{10,12},{12,10},{14,8},{1,7},{3,5},... | collective-permute-start | bytes 786440 | tf_op jit(solution)/shard_map/ppermute | solution.py:297
  16.3 0.0 collective-permute-done.6.refs_7_
  16.3 23.6 %collective-permute-start.1 = (f32[2,32,1024]{2,1,0:T(8,128)S(1)}, f32[2,32,1024]{2,1,0:T(8,128)S(1)}, u32[]{:S(2)}, u32[]{:S(2)}) collective-permute-start(f32[2,32,1024]{2,1,0:T(8,128)S(1)} %bitcast.13), channel_id=1, source_target_pairs={{0,4},{2,6},{4,0},{6,2},{8,12},{10,14},{12,8},{14,10},{1,5},{3,7},... | collective-permute-start | bytes 786440 | tf_op jit(solution)/shard_map/ppermute | solution.py:297
  39.9 0.0 collective-permute-done.5.refs_6_
  39.9 1.6 collective-permute-start
  41.5 8.2 %collective-permute-done.4.refs_5_ = f32[2,32,1024]{2,1,0:T(8,128)S(1)} collective-permute-done((f32[2,32,1024]{2,1,0:T(8,128)S(1)}, f32[2,32,1024]{2,1,0:T(8,128)S(1)}, u32[]{:S(2)}, u32[]{:S(2)}) %collective-permute-start.4) | collective-permute-done | bytes 262176 | tf_op jit(solution)/shard_map/ppermute | solution.py:297
  49.8 0.0 collective-permute-start.14
  49.8 5.1 %collective-permute-done.3.refs_4_ = f32[2,32,1024]{2,1,0:T(8,128)S(1)} collective-permute-done((f32[2,32,1024]{2,1,0:T(8,128)S(1)}, f32[2,32,1024]{2,1,0:T(8,128)S(1)}, u32[]{:S(2)}, u32[]{:S(2)}) %collective-permute-start.3) | collective-permute-done | bytes 262176 | tf_op jit(solution)/shard_map/ppermute | solution.py:297
  54.9 0.7 pad_maximum_fusion.signs
  55.6 0.4 collective-permute-start.12
  56.0 0.4 collective-permute-done.1.refs_2_
  56.4 0.5 collective-permute-start.10
  56.9 0.0 collective-permute-done.14.refs_15_
  56.9 0.1 collective-permute-start.9
  57.0 0.4 collective-permute-start.8
  57.5 0.2 copy-done.9
  57.6 0.1 copy-done.10
  57.8 0.6 pad_add_fusion.1.info
  58.4 0.1 eq.24
  58.5 0.8 compare_convert_fusion.refs_16_
  59.2 0.0 collective-permute-done.12.refs_13_
  59.3 0.0 collective-permute-done.11.refs_12_
  59.3 0.0 collective-permute-done.9.refs_10_
  59.4 0.6 copy-done.11
  60.0 0.1 copy-done.12
  60.1 0.1 copy-done.13
  60.2 0.7 copy-done.14
  60.8 80.7 %pair_coefficients.1 = (bf16[5120,384]{1,0:T(8,128)(2,1)}, bf16[4096,384]{1,0:T(8,128)(2,1)}) custom-call(s32[2]{0:T(128)} %pad_add_fusion.1.info, s32[9216]{0:T(1024)} %pad_add_fusion.cells, f32[9216]{0:T(1024)} %pad_maximum_fusion.signs, f32[2,32,1024]{2,1,0:T(8,128)} %bitcast.15, f32[2,32,1024]{2,1,0:T(8,128)} %copy-done.8, f32[2,32,1024]{2,1,0:T(8,128)} %copy-done.7, ...), custom_call_target="tpu_custom_call" | custom-call | flops 30000001024 | bytes 12000000 | tf_op jit(solution)/shard_map/pair_coefficients/pallas_call | solution.py:141
  141.5 0.5 collective-permute-start.15
  142.0 6.8 %collective-permute-done.15.recv.recv_g = bf16[5120,384]{1,0:T(8,128)(2,1)} collective-permute-done((bf16[5120,384]{1,0:T(8,128)(2,1)}, bf16[5120,384]{1,0:T(8,128)(2,1)}, u32[]{:S(2)}, u32[]{:S(2)}) %collective-permute-start.15) | collective-permute-done | bytes 3932192 | tf_op jit(solution)/shard_map/ppermute | solution.py:318
  148.8 39.1 %coulomb_partial.1 = (f32[8,2,2,24,384]{4,3,2,1,0:T(8,128)}, f32[8,2,2,24,384]{4,3,2,1,0:T(8,128)}) custom-call(s32[2]{0:T(128)} %pad_add_fusion.1.info, bf16[4096,384]{1,0:T(8,128)(2,1)} %get-tuple-element.9.keep, bf16[5120,384]{1,0:T(8,128)(2,1)} %get-tuple-element.10.send_g, bf16[5120,384]{1,0:T(8,128)(2,1)} %collective-permute-done.15.recv.recv_g, ...), custom_call_target="tpu_custom_call" | custom-call | flops 28000000000 | bytes 45000000 | tf_op jit(solution)/shard_map/coulomb_partial/pallas_call | solution.py:249
  187.8 0.4 collective-permute-start.16
  188.2 2.7 %collective-permute-done.16 = f32[8,2,2,24,384]{4,3,2,1,0:T(8,128)S(1)} collective-permute-done((f32[8,2,2,24,384]{4,3,2,1,0:T(8,128)}, f32[8,2,2,24,384]{4,3,2,1,0:T(8,128)S(1)}, u32[]{:S(2)}, u32[]{:S(2)}) %collective-permute-start.16) | collective-permute-done | bytes 1179680 | tf_op jit(solution)/shard_map/ppermute | solution.py:322
  190.9 1.4 add_convert_fusion
  192.3 21.2 %all_to_all.5 = bf16[8,2,2,24,384]{4,3,2,1,0:T(8,128)(2,1)S(1)} all-to-all(bf16[8,2,2,24,384]{4,3,2,1,0:T(8,128)(2,1)S(1)} %add_convert_fusion), channel_id=1, replica_groups=mesh['kpt'=2,'row'=8,'col'=2] {'row'}, dimensions={0} | all-to-all | bytes 1179648 | tf_op jit(solution)/shard_map/all_to_all | solution.py:323
  213.6 0.7 convert_reduce_fusion
  (37 shorter events, 0.1 us)
Async XLA Ops:
  1.0 38.9 %copy-start = (f32[32,2,1024]{2,0,1:T(8,128)}, f32[32,2,1024]{2,0,1:T(8,128)S(1)}, u32[]{:S(2)}) copy-start(f32[32,2,1024]{2,0,1:T(8,128)S(1)} %copy.11) | copy-start | bytes 786436
  1.0 13.0 %collective-permute-start.7 = (f32[2,32,1024]{2,1,0:T(8,128)S(1)}, f32[2,32,1024]{2,1,0:T(8,128)S(1)}, u32[]{:S(2)}, u32[]{:S(2)}) collective-permute-start(f32[2,32,1024]{2,1,0:T(8,128)S(1)} %bitcast.7), channel_id=1, source_target_pairs={{0,1},{1,0},{2,3},{3,2},{4,5},{5,4},{6,7},{7,6},{8,9},{9,8},{10,11... | collective-permute-start | bytes 786440 | tf_op jit(solution)/shard_map/ppermute | solution.py:298
  1.6 14.7 %collective-permute-start.6 = (f32[2,32,1024]{2,1,0:T(8,128)S(1)}, f32[2,32,1024]{2,1,0:T(8,128)S(1)}, u32[]{:S(2)}, u32[]{:S(2)}) collective-permute-start(f32[2,32,1024]{2,1,0:T(8,128)S(1)} %bitcast.8), channel_id=1, source_target_pairs={{0,14},{2,12},{4,10},{6,8},{8,6},{10,4},{12,2},{14,0},{1,15},{3,13... | collective-permute-start | bytes 786440 | tf_op jit(solution)/shard_map/ppermute | solution.py:297
  7.2 32.7 %collective-permute-start.5 = (f32[2,32,1024]{2,1,0:T(8,128)S(1)}, f32[2,32,1024]{2,1,0:T(8,128)S(1)}, u32[]{:S(2)}, u32[]{:S(2)}) collective-permute-start(f32[2,32,1024]{2,1,0:T(8,128)S(1)} %bitcast.9), channel_id=1, source_target_pairs={{0,12},{2,14},{4,8},{6,10},{8,4},{10,6},{12,0},{14,2},{1,13},{3,15... | collective-permute-start | bytes 786440 | tf_op jit(solution)/shard_map/ppermute | solution.py:297
  7.4 42.3 %collective-permute-start.4 = (f32[2,32,1024]{2,1,0:T(8,128)S(1)}, f32[2,32,1024]{2,1,0:T(8,128)S(1)}, u32[]{:S(2)}, u32[]{:S(2)}) collective-permute-start(f32[2,32,1024]{2,1,0:T(8,128)S(1)} %bitcast.10), channel_id=1, source_target_pairs={{0,10},{2,8},{4,14},{6,12},{8,2},{10,0},{12,6},{14,4},{1,11},{3,9}... | collective-permute-start | bytes 786440 | tf_op jit(solution)/shard_map/ppermute | solution.py:297
  8.2 46.7 %collective-permute-start.3 = (f32[2,32,1024]{2,1,0:T(8,128)S(1)}, f32[2,32,1024]{2,1,0:T(8,128)S(1)}, u32[]{:S(2)}, u32[]{:S(2)}) collective-permute-start(f32[2,32,1024]{2,1,0:T(8,128)S(1)} %bitcast.11), channel_id=1, source_target_pairs={{0,8},{2,10},{4,12},{6,14},{8,0},{10,2},{12,4},{14,6},{1,9},{3,11}... | collective-permute-start | bytes 786440 | tf_op jit(solution)/shard_map/ppermute | solution.py:297
  14.0 45.2 %copy-start.1 = (f32[2,32,1024]{2,1,0:T(8,128)}, f32[2,32,1024]{2,1,0:T(8,128)S(1)}, u32[]{:S(2)}) copy-start(f32[2,32,1024]{2,1,0:T(8,128)S(1)} %collective-permute-done.7.refs_8_) | copy-start | bytes 786436
  14.0 41.6 %collective-permute-start.2 = (f32[2,32,1024]{2,1,0:T(8,128)S(1)}, f32[2,32,1024]{2,1,0:T(8,128)S(1)}, u32[]{:S(2)}, u32[]{:S(2)}) collective-permute-start(f32[2,32,1024]{2,1,0:T(8,128)S(1)} %bitcast.12), channel_id=1, source_target_pairs={{0,6},{2,4},{4,2},{6,0},{8,14},{10,12},{12,10},{14,8},{1,7},{3,5},... | collective-permute-start | bytes 786440 | tf_op jit(solution)/shard_map/ppermute | solution.py:297
  16.3 43.0 %copy-start.2 = (f32[2,32,1024]{2,1,0:T(8,128)}, f32[2,32,1024]{2,1,0:T(8,128)S(1)}, u32[]{:S(2)}) copy-start(f32[2,32,1024]{2,1,0:T(8,128)S(1)} %collective-permute-done.6.refs_7_) | copy-start | bytes 786436
  16.3 40.1 %collective-permute-start.1 = (f32[2,32,1024]{2,1,0:T(8,128)S(1)}, f32[2,32,1024]{2,1,0:T(8,128)S(1)}, u32[]{:S(2)}, u32[]{:S(2)}) collective-permute-start(f32[2,32,1024]{2,1,0:T(8,128)S(1)} %bitcast.13), channel_id=1, source_target_pairs={{0,4},{2,6},{4,0},{6,2},{8,12},{10,14},{12,8},{14,10},{1,5},{3,7},... | collective-permute-start | bytes 786440 | tf_op jit(solution)/shard_map/ppermute | solution.py:297
  39.9 19.4 %copy-start.3 = (f32[2,32,1024]{2,1,0:T(8,128)}, f32[2,32,1024]{2,1,0:T(8,128)S(1)}, u32[]{:S(2)}) copy-start(f32[2,32,1024]{2,1,0:T(8,128)S(1)} %collective-permute-done.5.refs_6_) | copy-start | bytes 786436
  39.9 16.5 %collective-permute-start = (f32[2,32,1024]{2,1,0:T(8,128)S(1)}, f32[2,32,1024]{2,1,0:T(8,128)S(1)}, u32[]{:S(2)}, u32[]{:S(2)}) collective-permute-start(f32[2,32,1024]{2,1,0:T(8,128)S(1)} %bitcast.14), channel_id=1, source_target_pairs={{0,2},{2,0},{4,6},{6,4},{8,10},{10,8},{12,14},{14,12},{1,3},{3,1},... | collective-permute-start | bytes 786440 | tf_op jit(solution)/shard_map/ppermute | solution.py:297
  49.7 9.6 %copy-start.4 = (f32[2,32,1024]{2,1,0:T(8,128)}, f32[2,32,1024]{2,1,0:T(8,128)S(1)}, u32[]{:S(2)}) copy-start(f32[2,32,1024]{2,1,0:T(8,128)S(1)} %collective-permute-done.4.refs_5_) | copy-start | bytes 786436
  49.8 7.2 %collective-permute-start.14 = (f32[2,32,1024]{2,1,0:T(8,128)S(1)}, f32[2,32,1024]{2,1,0:T(8,128)S(1)}, u32[]{:S(2)}, u32[]{:S(2)}) collective-permute-start(f32[2,32,1024]{2,1,0:T(8,128)S(1)} %collective-permute-done.6.refs_7_), channel_id=1, source_target_pairs={{0,1},{1,0},{2,3},{3,2},{4,5},{5,4},{6,7},{7,6},{8,9},{9,8},{10,11... | collective-permute-start | bytes 786440 | tf_op jit(solution)/shard_map/ppermute | solution.py:298
  54.9 4.5 %copy-start.5 = (f32[2,32,1024]{2,1,0:T(8,128)}, f32[2,32,1024]{2,1,0:T(8,128)S(1)}, u32[]{:S(2)}) copy-start(f32[2,32,1024]{2,1,0:T(8,128)S(1)} %collective-permute-done.3.refs_4_) | copy-start | bytes 786436
  54.9 2.2 %collective-permute-start.13 = (f32[2,32,1024]{2,1,0:T(8,128)S(1)}, f32[2,32,1024]{2,1,0:T(8,128)S(1)}, u32[]{:S(2)}, u32[]{:S(2)}) collective-permute-start(f32[2,32,1024]{2,1,0:T(8,128)S(1)} %collective-permute-done.5.refs_6_), channel_id=1, source_target_pairs={{0,1},{1,0},{2,3},{3,2},{4,5},{5,4},{6,7},{7,6},{8,9},{9,8},{10,11... | collective-permute-start | bytes 786440 | tf_op jit(solution)/shard_map/ppermute | solution.py:298
  55.6 3.8 %copy-start.6 = (f32[2,32,1024]{2,1,0:T(8,128)}, f32[2,32,1024]{2,1,0:T(8,128)S(1)}, u32[]{:S(2)}) copy-start(f32[2,32,1024]{2,1,0:T(8,128)S(1)} %collective-permute-done.2.refs_3_) | copy-start | bytes 786436
  55.6 3.7 %collective-permute-start.12 = (f32[2,32,1024]{2,1,0:T(8,128)S(1)}, f32[2,32,1024]{2,1,0:T(8,128)S(1)}, u32[]{:S(2)}, u32[]{:S(2)}) collective-permute-start(f32[2,32,1024]{2,1,0:T(8,128)S(1)} %collective-permute-done.4.refs_5_), channel_id=1, source_target_pairs={{0,1},{1,0},{2,3},{3,2},{4,5},{5,4},{6,7},{7,6},{8,9},{9,8},{10,11... | collective-permute-start | bytes 786440 | tf_op jit(solution)/shard_map/ppermute | solution.py:298
  56.4 2.9 %copy-start.7 = (f32[2,32,1024]{2,1,0:T(8,128)}, f32[2,32,1024]{2,1,0:T(8,128)S(1)}, u32[]{:S(2)}) copy-start(f32[2,32,1024]{2,1,0:T(8,128)S(1)} %collective-permute-done.1.refs_2_) | copy-start | bytes 786436
  56.4 2.8 %collective-permute-start.11 = (f32[2,32,1024]{2,1,0:T(8,128)S(1)}, f32[2,32,1024]{2,1,0:T(8,128)S(1)}, u32[]{:S(2)}, u32[]{:S(2)}) collective-permute-start(f32[2,32,1024]{2,1,0:T(8,128)S(1)} %collective-permute-done.3.refs_4_), channel_id=1, source_target_pairs={{0,1},{1,0},{2,3},{3,2},{4,5},{5,4},{6,7},{7,6},{8,9},{9,8},{10,11... | collective-permute-start | bytes 786440 | tf_op jit(solution)/shard_map/ppermute | solution.py:298
  56.4 2.9 %copy-start.8 = (f32[2,32,1024]{2,1,0:T(8,128)}, f32[2,32,1024]{2,1,0:T(8,128)S(1)}, u32[]{:S(2)}) copy-start(f32[2,32,1024]{2,1,0:T(8,128)S(1)} %collective-permute-done.refs_1_) | copy-start | bytes 786436
  56.4 2.9 %collective-permute-start.10 = (f32[2,32,1024]{2,1,0:T(8,128)S(1)}, f32[2,32,1024]{2,1,0:T(8,128)S(1)}, u32[]{:S(2)}, u32[]{:S(2)}) collective-permute-start(f32[2,32,1024]{2,1,0:T(8,128)S(1)} %collective-permute-done.2.refs_3_), channel_id=1, source_target_pairs={{0,1},{1,0},{2,3},{3,2},{4,5},{5,4},{6,7},{7,6},{8,9},{9,8},{10,11... | collective-permute-start | bytes 786440 | tf_op jit(solution)/shard_map/ppermute | solution.py:298
  56.9 0.7 copy-start.9
  56.9 2.4 %collective-permute-start.9 = (f32[2,32,1024]{2,1,0:T(8,128)S(1)}, f32[2,32,1024]{2,1,0:T(8,128)S(1)}, u32[]{:S(2)}, u32[]{:S(2)}) collective-permute-start(f32[2,32,1024]{2,1,0:T(8,128)S(1)} %collective-permute-done.1.refs_2_), channel_id=1, source_target_pairs={{0,1},{1,0},{2,3},{3,2},{4,5},{5,4},{6,7},{7,6},{8,9},{9,8},{10,11... | collective-permute-start | bytes 786440 | tf_op jit(solution)/shard_map/ppermute | solution.py:298
  57.0 0.7 copy-start.10
  57.0 3.8 %collective-permute-start.8 = (f32[2,32,1024]{2,1,0:T(8,128)S(1)}, f32[2,32,1024]{2,1,0:T(8,128)}, u32[]{:S(2)}, u32[]{:S(2)}) collective-permute-start(f32[2,32,1024]{2,1,0:T(8,128)S(1)} %collective-permute-done.refs_1_), channel_id=1, source_target_pairs={{0,1},{1,0},{2,3},{3,2},{4,5},{5,4},{6,7},{7,6},{8,9},{9,8},{10,11... | collective-permute-start | bytes 786440 | tf_op jit(solution)/shard_map/ppermute | solution.py:298
  59.3 0.7 copy-start.11
  59.3 0.8 copy-start.12
  59.3 0.8 copy-start.13
  60.1 0.7 copy-start.14
  141.5 7.2 %collective-permute-start.15 = (bf16[5120,384]{1,0:T(8,128)(2,1)}, bf16[5120,384]{1,0:T(8,128)(2,1)}, u32[]{:S(2)}, u32[]{:S(2)}) collective-permute-start(bf16[5120,384]{1,0:T(8,128)(2,1)} %get-tuple-element.10.send_g), channel_id=1, source_target_pairs={{0,1},{1,0},{2,3},{3,2},{4,5},{5,4},{6,7},{7,6},{8,9},{9,8},{10,11... | collective-permute-start | bytes 11796488 | tf_op jit(solution)/shard_map/ppermute | solution.py:318
  187.8 3.1 %collective-permute-start.16 = (f32[8,2,2,24,384]{4,3,2,1,0:T(8,128)}, f32[8,2,2,24,384]{4,3,2,1,0:T(8,128)S(1)}, u32[]{:S(2)}, u32[]{:S(2)}) collective-permute-start(f32[8,2,2,24,384]{4,3,2,1,0:T(8,128)} %get-tuple-element.12), channel_id=1, source_target_pairs={{0,1},{1,0},{2,3},{3,2},{4,5},{5,4},{6,7},{7,6},{8,9},{9,8},{10,11... | collective-permute-start | bytes 3538952 | tf_op jit(solution)/shard_map/ppermute | solution.py:322

commit v2 on v1

--- a/solution.py
+++ b/solution.py
@@ -106,23 +106,31 @@
         lines = dot_nn(xt[...], mid2[kq].reshape(8 * side, lanes))
         n = 4 * side
         re, im = lines[:n], lines[n:]
-        last = jnp.where(left, re[:, 128:], im[:, 128:])
-        spec[pl.ds(kq * n, n), 0, :] = jnp.concatenate([re[:, :128], im[:, :128], last], axis=1)
+        thirds = (re[:, :128], im[:, :128], jnp.where(left, re[:, 128:], im[:, 128:]))
+        for third in range(3):
+            for odd in range(2):
+                at = pl.ds(kq * 3 * n + 2 * third + odd, n // 2, stride=6)
+                spec[at, :] = thirds[third][odd * n // 2 : (odd + 1) * n // 2]
         return carry
 
-    lax.fori_loop(0, mid2.shape[0], column, 0, unroll=2)
-
-    block = stage.shape[0]
-    lane = lax.broadcasted_iota(jnp.int32, (1, 384), 1)
-    imag = ((lane >= 128) & (lane < 256)) | (lane >= 320)
+    lax.fori_loop(0, mid2.shape[0], column, 0, unroll=4)
+
+    block = 128
 
     def gather_into(out, first):
         def step(b, carry):
             base = first + b * block
             for j in range(block):
-                row = spec[cells[base + j]]
-                stage[j] = row * jnp.where(imag, signs[base + j], norm)
-            out[pl.ds(pl.multiple_of(b * block, block), block), :] = stage[:, 0, :].astype(BF)
+                odd, even = divmod(j, block // 2)
+                stage[pl.ds(6 * even + odd, 3, stride=2), :] = spec[pl.ds(cells[base + j], 3, stride=2), :]
+            sign = jnp.transpose(jnp.broadcast_to(signs[pl.ds(first // block + b, 1), :], (block, block)))
+            plain = jnp.full_like(sign, norm)
+            scales = (plain, sign, jnp.where(left, plain, sign))
+            at = pl.ds(pl.multiple_of(b * block, block), block)
+            for third in range(3):
+                halves = [stage[pl.ds(2 * third + odd, block // 2, stride=6), :] for odd in range(2)]
+                whole = jnp.concatenate(halves, axis=0) * scales[third]
+                out[at, third * 128 : (third + 1) * 128] = whole.astype(BF)
             return carry
 
         lax.fori_loop(0, out.shape[0] // block, step, 0)
@@ -144,14 +152,14 @@
             jax.ShapeDtypeStruct((send_rows, 384), BF),
             jax.ShapeDtypeStruct((keep_rows, 384), BF),
         ),
-        in_specs=[smem] * 3 + [pl.BlockSpec(memory_space=pl.ANY)] * len(pieces) + [vmem] * 5,
+        in_specs=[smem, smem, vmem] + [pl.BlockSpec(memory_space=pl.ANY)] * len(pieces) + [vmem] * 5,
         out_specs=(vmem, vmem),
         scratch_shapes=[
             pltpu.VMEM((side, members, side * side), F32),
             pltpu.VMEM((2, half, side // 8, 16, lanes), BF),
             pltpu.VMEM((half * side // 4, side // 2, 16, lanes), BF),
-            pltpu.VMEM((half * side * side, 1, 384), F32),
-            pltpu.VMEM((32, 1, 384), F32),
+            pltpu.VMEM((half * side * side * 3, 128), F32),
+            pltpu.VMEM((3 * 128, 128), F32),
             pltpu.SemaphoreType.DMA((len(pieces),)),
         ],
         compiler_params=pltpu.CompilerParams(vmem_limit_bytes=VMEM_BYTES),
@@ -159,7 +167,7 @@
             flops=30_000_000_000, bytes_accessed=12_000_000, transcendentals=0
         ),
         name="pair_coefficients",
-    )(info, cells, signs, *pieces, picks, *stage_tables(side))
+    )(info, cells, signs.reshape(-1, 128), *pieces, picks, *stage_tables(side))
 
 
 def ordered(mine, theirs, is_first):
@@ -277,7 +285,8 @@
     kx, ky, kz = gmap // (side * side), gmap // side % side, gmap % side
     mirrored = kz > side // 2
     kx, ky, kz = (jnp.where(mirrored, -k % side, k) for k in (kx, ky, kz))
-    cells = ((kz * (side // 4) + ky // 4) * side + kx) * 4 + ky % 4
+    place = kx * 4 + ky % 4
+    cells = (kz * (side // 4) + ky // 4) * 12 * side + place % (2 * side) * 6 + place // (2 * side)
     return cells, jnp.where(mirrored, -norm, norm).astype(F32)
 
 
@@ -293,8 +302,13 @@
 
     local = wannier.transpose(1, 0, 2)
     same = [local]
-    for shift in range(1, rows):
-        same.append(lax.ppermute(local, "row", [(i, i ^ shift) for i in range(rows)]))
+    for bit in reversed(range(log2(rows))):
+        hop = [(i, i ^ (1 << bit)) for i in range(rows)]
+        same += [lax.ppermute(piece, "row", hop) for piece in same]
+    order = [0]
+    for bit in reversed(range(log2(rows))):
+        order += [index ^ (1 << bit) for index in order]
+    same = [same[order.index(shift)] for shift in range(rows)]
     cross = [lax.ppermute(piece, "col", swap) for piece in same]
 
     wide = count // 3

time: 215 us -> 169 us (0.79)
  Pallas kernels: 120 us -> 91.3 us
  starting transfers between devices: 39 us -> 12.9 us
  waiting for transfers between devices: 23.3 us -> 31.1 us
    pallas_call x1, Pallas kernels: 80.7 us -> 52.2 us  [pair_coefficients(): pl.pallas_call(functools.partial(pair_kernel, side, planes, len(pieces) /...]
    ppermute x7, starting transfers between devices: 36.1 us -> 10.8 us  [shards(): same += [lax.ppermute(piece, 'row', hop) for piece in same]]
    ppermute x7, waiting for transfers between devices: 13.8 us -> 21.6 us  [shards(): same += [lax.ppermute(piece, 'row', hop) for piece in same]]
  transfers between devices with their start and end apart: 17 -> 17, of which waited for: 5 -> 7; matrix products, arithmetic and copies ran while one was open for 3% -> 3% of each run, Pallas kernels for 0% -> 0%
where the time goes in v2:
time: 169 us
  Pallas kernels  91.3 us (54%)
  waiting for transfers between devices  31.1 us (18%)
  blocking collectives  22.5 us (13%)
  starting transfers between devices  12.9 us (8%)
  other arithmetic  6.51 us (4%)
  local copies, waits for them, and re-layouts  4.07 us (2%)
    pallas_call x1, Pallas kernels, pair_coefficients(): pl.pallas_call(functools.partial(pair_kernel, side, planes, len(pieces) /...  52.2 us
    pallas_call x1, Pallas kernels, coulomb_partial(): pl.pallas_call(functools.partial(coulomb_kernel, steps, shares, scale), g...  39.1 us
    all_to_all x1, blocking collectives, shards(): lax.all_to_all(chip.astype(BF), 'row', split_axis=0, concat_axis=0, tiled...  22.5 us
    ppermute x7, waiting for transfers between devices, shards(): same += [lax.ppermute(piece, 'row', hop) for piece in same]  21.6 us
    ppermute x7, starting transfers between devices, shards(): same += [lax.ppermute(piece, 'row', hop) for piece in same]  10.8 us
    ppermute x1, waiting for transfers between devices, shards(): recv = lax.ppermute(send, 'col', swap)  6.75 us
  transfers between devices with their start and end apart: 17, of which 7 were waited for; matrix products, arithmetic and copies ran while one was open for 3% of the time, Pallas kernels for 0%

profile of v2, /device:TPU:0, one launch (start us, length us, event | category | flops | bytes accessed | tf_op | source)
XLA Modules:
  0.0 168.5 jit_solution(10321428670964037494)
XLA Ops:
  0.0 1.0 copy.11
  1.0 0.6 collective-permute-start.7
  1.6 3.7 %collective-permute-start.3 = (f32[2,32,1024]{2,1,0:T(8,128)S(1)}, f32[2,32,1024]{2,1,0:T(8,128)S(1)}, u32[]{:S(2)}, u32[]{:S(2)}) collective-permute-start(f32[2,32,1024]{2,1,0:T(8,128)S(1)} %bitcast.10), channel_id=1, source_target_pairs={{0,8},{2,10},{4,12},{6,14},{8,0},{10,2},{12,4},{14,6},{1,9},{3,11}... | collective-permute-start | bytes 786440 | tf_op jit(solution)/shard_map/ppermute | solution.py:307
  5.3 1.6 collective-permute-start.1
  6.8 1.5 collective-permute-start
  8.4 0.8 compare_select_fusion
  9.1 0.8 constant_dynamic-slice_fusion
  9.9 0.7 constant_dynamic-slice_fusion.1
  10.6 0.9 fusion.8
  11.5 6.4 %collective-permute-done.3.refs_4_ = f32[2,32,1024]{2,1,0:T(8,128)S(1)} collective-permute-done((f32[2,32,1024]{2,1,0:T(8,128)S(1)}, f32[2,32,1024]{2,1,0:T(8,128)S(1)}, u32[]{:S(2)}, u32[]{:S(2)}) %collective-permute-start.3) | collective-permute-done | bytes 262176 | tf_op jit(solution)/shard_map/ppermute | solution.py:307
  17.9 0.6 collective-permute-start.5
  18.5 0.6 maximum_bitcast_fusion.signs
  19.1 0.0 collective-permute-start.11
  19.1 0.0 collective-permute-done.7.refs_8_
  19.2 1.6 collective-permute-start.4
  20.7 0.0 collective-permute-done.1.refs_2_
  20.7 0.2 collective-permute-start.9
  20.9 0.0 collective-permute-done.refs_1_
  20.9 0.5 collective-permute-start.2
  21.4 4.5 %collective-permute-done.5.refs_6_ = f32[2,32,1024]{2,1,0:T(8,128)S(1)} collective-permute-done((f32[2,32,1024]{2,1,0:T(8,128)S(1)}, f32[2,32,1024]{2,1,0:T(8,128)S(1)}, u32[]{:S(2)}, u32[]{:S(2)}) %collective-permute-start.5) | collective-permute-done | bytes 262176 | tf_op jit(solution)/shard_map/ppermute | solution.py:307
  25.9 1.3 collective-permute-start.6
  27.2 0.6 pad_add_fusion.cells
  27.8 0.0 collective-permute-done.11.refs_12_
  27.8 0.0 collective-permute-start.8
  27.8 0.6 collective-permute-done.4.refs_5_
  28.4 0.5 collective-permute-start.12
  28.9 5.1 %collective-permute-done.2.refs_3_ = f32[2,32,1024]{2,1,0:T(8,128)S(1)} collective-permute-done((f32[2,32,1024]{2,1,0:T(8,128)S(1)}, f32[2,32,1024]{2,1,0:T(8,128)S(1)}, u32[]{:S(2)}, u32[]{:S(2)}) %collective-permute-start.2) | collective-permute-done | bytes 262176 | tf_op jit(solution)/shard_map/ppermute | solution.py:307
  34.0 0.0 collective-permute-start.10
  34.0 5.1 %collective-permute-done.6.refs_7_ = f32[2,32,1024]{2,1,0:T(8,128)S(1)} collective-permute-done((f32[2,32,1024]{2,1,0:T(8,128)S(1)}, f32[2,32,1024]{2,1,0:T(8,128)S(1)}, u32[]{:S(2)}, u32[]{:S(2)}) %collective-permute-start.6) | collective-permute-done | bytes 262176 | tf_op jit(solution)/shard_map/ppermute | solution.py:307
  39.1 0.6 pad_add_fusion.1.info
  39.8 0.1 eq.25
  39.9 0.8 compare_convert_fusion.refs_16_
  40.6 0.0 collective-permute-done.13.refs_14_
  40.7 0.0 collective-permute-done.12.refs_13_
  40.7 0.6 copy-done.11
  41.3 0.1 copy-done.12
  41.4 0.1 copy-done.13
  41.5 0.7 copy-done.14
  42.2 0.0 collective-permute-done.14.refs_15_
  42.2 52.2 %pair_coefficients.1 = (bf16[5120,384]{1,0:T(8,128)(2,1)}, bf16[4096,384]{1,0:T(8,128)(2,1)}) custom-call(s32[2]{0:T(128)} %pad_add_fusion.1.info, s32[9216]{0:T(1024)} %pad_add_fusion.cells, f32[72,128]{1,0:T(8,128)} %maximum_bitcast_fusion.signs, f32[2,32,1024]{2,1,0:T(8,128)} %bitcast.13, f32[2,32,1024]{2,1,0:T(8,128)} %copy-done.4, ...), custom_call_target="tpu_custom_call" | custom-call | flops 30000001024 | bytes 12000000 | tf_op jit(solution)/shard_map/pair_coefficients/pallas_call | solution.py:149
  94.4 0.6 collective-permute-start.15
  95.0 6.8 %collective-permute-done.15.recv.recv_g = bf16[5120,384]{1,0:T(8,128)(2,1)} collective-permute-done((bf16[5120,384]{1,0:T(8,128)(2,1)}, bf16[5120,384]{1,0:T(8,128)(2,1)}, u32[]{:S(2)}, u32[]{:S(2)}) %collective-permute-start.15) | collective-permute-done | bytes 3932192 | tf_op jit(solution)/shard_map/ppermute | solution.py:332
  101.7 39.1 %coulomb_partial.1 = (f32[8,2,2,24,384]{4,3,2,1,0:T(8,128)}, f32[8,2,2,24,384]{4,3,2,1,0:T(8,128)}) custom-call(s32[2]{0:T(128)} %pad_add_fusion.1.info, bf16[4096,384]{1,0:T(8,128)(2,1)} %get-tuple-element.9.keep, bf16[5120,384]{1,0:T(8,128)(2,1)} %get-tuple-element.10.send_g, bf16[5120,384]{1,0:T(8,128)(2,1)} %collective-permute-done.15.recv.recv_g, ...), custom_call_target="tpu_custom_call" | custom-call | flops 28000000000 | bytes 45000000 | tf_op jit(solution)/shard_map/coulomb_partial/pallas_call | solution.py:257
  140.8 0.4 collective-permute-start.16
  141.2 2.7 %collective-permute-done.16 = f32[8,2,2,24,384]{4,3,2,1,0:T(8,128)S(1)} collective-permute-done((f32[8,2,2,24,384]{4,3,2,1,0:T(8,128)}, f32[8,2,2,24,384]{4,3,2,1,0:T(8,128)S(1)}, u32[]{:S(2)}, u32[]{:S(2)}) %collective-permute-start.16) | collective-permute-done | bytes 1179680 | tf_op jit(solution)/shard_map/ppermute | solution.py:336
  143.9 1.4 add_convert_fusion
  145.3 22.5 %all_to_all.5 = bf16[8,2,2,24,384]{4,3,2,1,0:T(8,128)(2,1)S(1)} all-to-all(bf16[8,2,2,24,384]{4,3,2,1,0:T(8,128)(2,1)S(1)} %add_convert_fusion), channel_id=1, replica_groups=mesh['kpt'=2,'row'=8,'col'=2] {'row'}, dimensions={0} | all-to-all | bytes 1179648 | tf_op jit(solution)/shard_map/all_to_all | solution.py:337
  167.8 0.7 convert_reduce_fusion
  (37 shorter events, 0.1 us)
Async XLA Ops:
  1.0 5.8 %copy-start = (f32[32,2,1024]{2,0,1:T(8,128)}, f32[32,2,1024]{2,0,1:T(8,128)S(1)}, u32[]{:S(2)}) copy-start(f32[32,2,1024]{2,0,1:T(8,128)S(1)} %copy.11) | copy-start | bytes 786436
  1.0 18.1 %collective-permute-start.7 = (f32[2,32,1024]{2,1,0:T(8,128)S(1)}, f32[2,32,1024]{2,1,0:T(8,128)S(1)}, u32[]{:S(2)}, u32[]{:S(2)}) collective-permute-start(f32[2,32,1024]{2,1,0:T(8,128)S(1)} %bitcast.9), channel_id=1, source_target_pairs={{0,1},{1,0},{2,3},{3,2},{4,5},{5,4},{6,7},{7,6},{8,9},{9,8},{10,11... | collective-permute-start | bytes 786440 | tf_op jit(solution)/shard_map/ppermute | solution.py:312
  1.6 16.3 %collective-permute-start.3 = (f32[2,32,1024]{2,1,0:T(8,128)S(1)}, f32[2,32,1024]{2,1,0:T(8,128)S(1)}, u32[]{:S(2)}, u32[]{:S(2)}) collective-permute-start(f32[2,32,1024]{2,1,0:T(8,128)S(1)} %bitcast.10), channel_id=1, source_target_pairs={{0,8},{2,10},{4,12},{6,14},{8,0},{10,2},{12,4},{14,6},{1,9},{3,11}... | collective-permute-start | bytes 786440 | tf_op jit(solution)/shard_map/ppermute | solution.py:307
  5.3 15.5 %collective-permute-start.1 = (f32[2,32,1024]{2,1,0:T(8,128)S(1)}, f32[2,32,1024]{2,1,0:T(8,128)S(1)}, u32[]{:S(2)}, u32[]{:S(2)}) collective-permute-start(f32[2,32,1024]{2,1,0:T(8,128)S(1)} %bitcast.11), channel_id=1, source_target_pairs={{0,4},{2,6},{4,0},{6,2},{8,12},{10,14},{12,8},{14,10},{1,5},{3,7},... | collective-permute-start | bytes 786440 | tf_op jit(solution)/shard_map/ppermute | solution.py:307
  6.8 14.1 %collective-permute-start = (f32[2,32,1024]{2,1,0:T(8,128)S(1)}, f32[2,32,1024]{2,1,0:T(8,128)S(1)}, u32[]{:S(2)}, u32[]{:S(2)}) collective-permute-start(f32[2,32,1024]{2,1,0:T(8,128)S(1)} %bitcast.12), channel_id=1, source_target_pairs={{0,2},{2,0},{4,6},{6,4},{8,10},{10,8},{12,14},{14,12},{1,3},{3,1},... | collective-permute-start | bytes 786440 | tf_op jit(solution)/shard_map/ppermute | solution.py:307
  17.9 22.7 %copy-start.2 = (f32[2,32,1024]{2,1,0:T(8,128)}, f32[2,32,1024]{2,1,0:T(8,128)S(1)}, u32[]{:S(2)}) copy-start(f32[2,32,1024]{2,1,0:T(8,128)S(1)} %collective-permute-done.3.refs_4_) | copy-start | bytes 786436
  17.9 8.0 %collective-permute-start.5 = (f32[2,32,1024]{2,1,0:T(8,128)S(1)}, f32[2,32,1024]{2,1,0:T(8,128)S(1)}, u32[]{:S(2)}, u32[]{:S(2)}) collective-permute-start(f32[2,32,1024]{2,1,0:T(8,128)S(1)} %collective-permute-done.3.refs_4_), channel_id=1, source_target_pairs={{0,4},{2,6},{4,0},{6,2},{8,12},{10,14},{12,8},{14,10},{1,5},{3,7},... | collective-permute-start | bytes 786440 | tf_op jit(solution)/shard_map/ppermute | solution.py:307
  19.1 8.7 %collective-permute-start.11 = (f32[2,32,1024]{2,1,0:T(8,128)S(1)}, f32[2,32,1024]{2,1,0:T(8,128)S(1)}, u32[]{:S(2)}, u32[]{:S(2)}) collective-permute-start(f32[2,32,1024]{2,1,0:T(8,128)S(1)} %collective-permute-done.3.refs_4_), channel_id=1, source_target_pairs={{0,1},{1,0},{2,3},{3,2},{4,5},{5,4},{6,7},{7,6},{8,9},{9,8},{10,11... | collective-permute-start | bytes 786440 | tf_op jit(solution)/shard_map/ppermute | solution.py:312
  19.1 21.5 %copy-start.1 = (f32[2,32,1024]{2,1,0:T(8,128)}, f32[2,32,1024]{2,1,0:T(8,128)S(1)}, u32[]{:S(2)}) copy-start(f32[2,32,1024]{2,1,0:T(8,128)S(1)} %collective-permute-done.7.refs_8_) | copy-start | bytes 786436
  19.2 9.2 %collective-permute-start.4 = (f32[2,32,1024]{2,1,0:T(8,128)S(1)}, f32[2,32,1024]{2,1,0:T(8,128)S(1)}, u32[]{:S(2)}, u32[]{:S(2)}) collective-permute-start(f32[2,32,1024]{2,1,0:T(8,128)S(1)} %collective-permute-done.3.refs_4_), channel_id=1, source_target_pairs={{0,2},{2,0},{4,6},{6,4},{8,10},{10,8},{12,14},{14,12},{1,3},{3,1},... | collective-permute-start | bytes 786440 | tf_op jit(solution)/shard_map/ppermute | solution.py:307
  20.7 19.9 %copy-start.3 = (f32[2,32,1024]{2,1,0:T(8,128)}, f32[2,32,1024]{2,1,0:T(8,128)S(1)}, u32[]{:S(2)}) copy-start(f32[2,32,1024]{2,1,0:T(8,128)S(1)} %collective-permute-done.1.refs_2_) | copy-start | bytes 786436
  20.7 7.7 %collective-permute-start.9 = (f32[2,32,1024]{2,1,0:T(8,128)S(1)}, f32[2,32,1024]{2,1,0:T(8,128)S(1)}, u32[]{:S(2)}, u32[]{:S(2)}) collective-permute-start(f32[2,32,1024]{2,1,0:T(8,128)S(1)} %collective-permute-done.1.refs_2_), channel_id=1, source_target_pairs={{0,1},{1,0},{2,3},{3,2},{4,5},{5,4},{6,7},{7,6},{8,9},{9,8},{10,11... | collective-permute-start | bytes 786440 | tf_op jit(solution)/shard_map/ppermute | solution.py:312
  20.9 19.8 %copy-start.4 = (f32[2,32,1024]{2,1,0:T(8,128)}, f32[2,32,1024]{2,1,0:T(8,128)S(1)}, u32[]{:S(2)}) copy-start(f32[2,32,1024]{2,1,0:T(8,128)S(1)} %collective-permute-done.refs_1_) | copy-start | bytes 786436
  20.9 13.1 %collective-permute-start.2 = (f32[2,32,1024]{2,1,0:T(8,128)S(1)}, f32[2,32,1024]{2,1,0:T(8,128)S(1)}, u32[]{:S(2)}, u32[]{:S(2)}) collective-permute-start(f32[2,32,1024]{2,1,0:T(8,128)S(1)} %collective-permute-done.1.refs_2_), channel_id=1, source_target_pairs={{0,2},{2,0},{4,6},{6,4},{8,10},{10,8},{12,14},{14,12},{1,3},{3,1},... | collective-permute-start | bytes 786440 | tf_op jit(solution)/shard_map/ppermute | solution.py:307
  25.9 14.8 %copy-start.5 = (f32[2,32,1024]{2,1,0:T(8,128)}, f32[2,32,1024]{2,1,0:T(8,128)S(1)}, u32[]{:S(2)}) copy-start(f32[2,32,1024]{2,1,0:T(8,128)S(1)} %collective-permute-done.5.refs_6_) | copy-start | bytes 786436
  25.9 13.2 %collective-permute-start.6 = (f32[2,32,1024]{2,1,0:T(8,128)S(1)}, f32[2,32,1024]{2,1,0:T(8,128)S(1)}, u32[]{:S(2)}, u32[]{:S(2)}) collective-permute-start(f32[2,32,1024]{2,1,0:T(8,128)S(1)} %collective-permute-done.5.refs_6_), channel_id=1, source_target_pairs={{0,2},{2,0},{4,6},{6,4},{8,10},{10,8},{12,14},{14,12},{1,3},{3,1},... | collective-permute-start | bytes 786440 | tf_op jit(solution)/shard_map/ppermute | solution.py:307
  27.8 11.3 %copy-start.6 = (f32[2,32,1024]{2,1,0:T(8,128)}, f32[2,32,1024]{2,1,0:T(8,128)S(1)}, u32[]{:S(2)}) copy-start(f32[2,32,1024]{2,1,0:T(8,128)S(1)} %collective-permute-done.11.refs_12_) | copy-start | bytes 786436
  27.8 12.8 %collective-permute-start.8 = (f32[2,32,1024]{2,1,0:T(8,128)S(1)}, f32[2,32,1024]{2,1,0:T(8,128)S(1)}, u32[]{:S(2)}, u32[]{:S(2)}) collective-permute-start(f32[2,32,1024]{2,1,0:T(8,128)S(1)} %collective-permute-done.refs_1_), channel_id=1, source_target_pairs={{0,1},{1,0},{2,3},{3,2},{4,5},{5,4},{6,7},{7,6},{8,9},{9,8},{10,11... | collective-permute-start | bytes 786440 | tf_op jit(solution)/shard_map/ppermute | solution.py:312
  28.4 12.3 %copy-start.7 = (f32[2,32,1024]{2,1,0:T(8,128)}, f32[2,32,1024]{2,1,0:T(8,128)S(1)}, u32[]{:S(2)}) copy-start(f32[2,32,1024]{2,1,0:T(8,128)S(1)} %collective-permute-done.4.refs_5_) | copy-start | bytes 786436
  28.4 12.2 %collective-permute-start.13 = (f32[2,32,1024]{2,1,0:T(8,128)S(1)}, f32[2,32,1024]{2,1,0:T(8,128)S(1)}, u32[]{:S(2)}, u32[]{:S(2)}) collective-permute-start(f32[2,32,1024]{2,1,0:T(8,128)S(1)} %collective-permute-done.5.refs_6_), channel_id=1, source_target_pairs={{0,1},{1,0},{2,3},{3,2},{4,5},{5,4},{6,7},{7,6},{8,9},{9,8},{10,11... | collective-permute-start | bytes 786440 | tf_op jit(solution)/shard_map/ppermute | solution.py:312
  28.4 10.7 %copy-start.8 = (f32[2,32,1024]{2,1,0:T(8,128)}, f32[2,32,1024]{2,1,0:T(8,128)S(1)}, u32[]{:S(2)}) copy-start(f32[2,32,1024]{2,1,0:T(8,128)S(1)} %collective-permute-done.9.refs_10_) | copy-start | bytes 786436
  28.4 12.3 %collective-permute-start.12 = (f32[2,32,1024]{2,1,0:T(8,128)S(1)}, f32[2,32,1024]{2,1,0:T(8,128)S(1)}, u32[]{:S(2)}, u32[]{:S(2)}) collective-permute-start(f32[2,32,1024]{2,1,0:T(8,128)S(1)} %collective-permute-done.4.refs_5_), channel_id=1, source_target_pairs={{0,1},{1,0},{2,3},{3,2},{4,5},{5,4},{6,7},{7,6},{8,9},{9,8},{10,11... | collective-permute-start | bytes 786440 | tf_op jit(solution)/shard_map/ppermute | solution.py:312
  34.0 6.7 %copy-start.9 = (f32[2,32,1024]{2,1,0:T(8,128)}, f32[2,32,1024]{2,1,0:T(8,128)S(1)}, u32[]{:S(2)}) copy-start(f32[2,32,1024]{2,1,0:T(8,128)S(1)} %collective-permute-done.2.refs_3_) | copy-start | bytes 786436
  34.0 6.7 %collective-permute-start.10 = (f32[2,32,1024]{2,1,0:T(8,128)S(1)}, f32[2,32,1024]{2,1,0:T(8,128)S(1)}, u32[]{:S(2)}, u32[]{:S(2)}) collective-permute-start(f32[2,32,1024]{2,1,0:T(8,128)S(1)} %collective-permute-done.2.refs_3_), channel_id=1, source_target_pairs={{0,1},{1,0},{2,3},{3,2},{4,5},{5,4},{6,7},{7,6},{8,9},{9,8},{10,11... | collective-permute-start | bytes 786440 | tf_op jit(solution)/shard_map/ppermute | solution.py:312
  39.1 1.6 copy-start.10
  39.1 3.1 %collective-permute-start.14 = (f32[2,32,1024]{2,1,0:T(8,128)S(1)}, f32[2,32,1024]{2,1,0:T(8,128)}, u32[]{:S(2)}, u32[]{:S(2)}) collective-permute-start(f32[2,32,1024]{2,1,0:T(8,128)S(1)} %collective-permute-done.6.refs_7_), channel_id=1, source_target_pairs={{0,1},{1,0},{2,3},{3,2},{4,5},{5,4},{6,7},{7,6},{8,9},{9,8},{10,11... | collective-permute-start | bytes 786440 | tf_op jit(solution)/shard_map/ppermute | solution.py:312
  40.6 0.7 copy-start.11
  40.7 0.8 copy-start.12
  40.7 0.8 copy-start.13
  41.5 0.7 copy-start.14
  94.4 7.3 %collective-permute-start.15 = (bf16[5120,384]{1,0:T(8,128)(2,1)}, bf16[5120,384]{1,0:T(8,128)(2,1)}, u32[]{:S(2)}, u32[]{:S(2)}) collective-permute-start(bf16[5120,384]{1,0:T(8,128)(2,1)} %get-tuple-element.10.send_g), channel_id=1, source_target_pairs={{0,1},{1,0},{2,3},{3,2},{4,5},{5,4},{6,7},{7,6},{8,9},{9,8},{10,11... | collective-permute-start | bytes 11796488 | tf_op jit(solution)/shard_map/ppermute | solution.py:332
  140.8 3.1 %collective-permute-start.16 = (f32[8,2,2,24,384]{4,3,2,1,0:T(8,128)}, f32[8,2,2,24,384]{4,3,2,1,0:T(8,128)S(1)}, u32[]{:S(2)}, u32[]{:S(2)}) collective-permute-start(f32[8,2,2,24,384]{4,3,2,1,0:T(8,128)} %get-tuple-element.12), channel_id=1, source_target_pairs={{0,1},{1,0},{2,3},{3,2},{4,5},{5,4},{6,7},{7,6},{8,9},{9,8},{10,11... | collective-permute-start | bytes 3538952 | tf_op jit(solution)/shard_map/ppermute | solution.py:336

commit v3 on v2

v3 whole, which is shorter than its diff:
```python
import functools
import math

import jax
import jax.numpy as jnp
import numpy as np
from jax import lax
from jax.experimental import pallas as pl
from jax.experimental.pallas import tpu as pltpu
from jax.sharding import PartitionSpec as P

BF = jnp.bfloat16
F32 = jnp.float32
SCALE = 1.62455
VMEM_BYTES = 67_043_328
CHUNKS = 4


def stage_tables(side):
    half = side // 2 + 1
    positions = np.arange(side)
    angles = 2.0 * np.pi * (np.outer(positions, positions) % side) / side
    cosine, sine = SCALE * np.cos(angles), SCALE * np.sin(angles)
    z_table = np.zeros((half, 2, 8, 8, side))
    for y in range(8):
        z_table[:, 0, y, y, :] = cosine[:half]
        z_table[:, 1, y, y, :] = -sine[:half]
    line = np.zeros((side, 2, side, 2))
    line[:, 0, :, 0] = cosine
    line[:, 0, :, 1] = sine
    line[:, 1, :, 0] = -sine
    line[:, 1, :, 1] = cosine
    y_one = line.reshape(side // 4, 4, 2, side // 8, 8, 2).transpose(0, 2, 1, 3, 5, 4)
    y_one = y_one.reshape(2 * side, 2 * side)
    x_four = np.einsum("koni,ab->okanib", line, np.eye(4)).reshape(8 * side, 8 * side)
    z_table = z_table.reshape(16 * half, 8 * side)
    tables = (z_table, np.kron(np.eye(4), y_one), y_one, x_four)
    return [jnp.asarray(table.astype(np.float32)).astype(BF) for table in tables]


def dot_nt(a, b):
    return lax.dot_general(a, b, (((1,), (1,)), ((), ())), preferred_element_type=F32)


def dot_nn(a, b):
    return lax.dot_general(a, b, (((1,), (0,)), ((), ())), preferred_element_type=F32)


def log2(n):
    return n.bit_length() - 1


def transform_planes(side, planes, my_col, pieces, tables, wann, mid1, sems, sink):
    picks, zt, yt, ys = [held for _, held in tables]
    half = side // 2 + 1
    lanes = mid1.shape[-1]
    own = lanes * 3 // 4
    shifts = len(pieces) // 2

    for index, piece in enumerate(pieces):
        at = pl.ds(index * planes, planes)
        pltpu.make_async_copy(piece, wann.at[at], sems.at[index]).start()
    loads = [
        pltpu.make_async_copy(table, held, sems.at[len(pieces) + index])
        for index, (table, held) in enumerate(tables)
    ]
    for load in loads:
        load.start()

    def arrived(index):
        at = pl.ds(index * planes, planes)
        pltpu.make_async_copy(pieces[0], wann.at[at], sems.at[index]).wait()

    def plane_pair(pair, carry):
        for h in range(2):
            x = 2 * pair + h
            shift = lax.shift_right_logical(x, log2(2 * planes))
            from_col = lax.shift_right_logical(x, log2(planes)) & 1
            index = (from_col ^ my_col) * shifts + shift
            if planes <= 2:
                if h % planes == 0:
                    arrived(index)
            else:
                pl.when(x & (planes - 1) == 0)(functools.partial(arrived, index))
            plane = wann[index * planes + (x & (planes - 1))]
            high = plane.astype(BF)
            low = (plane - high.astype(F32)).astype(BF)
            both = dot_nn(picks[...], jnp.concatenate([high, low], axis=0))
            density = (both[:own] * both[own:]).astype(BF)
            density = jnp.concatenate([density, density[lanes // 2 : own]], axis=0)
            for t in range(side // 8):
                lines = dot_nt(zt[...], density[:, t * 8 * side : (t + 1) * 8 * side])
                mid1[h, :, t] = lines.astype(BF).reshape(half, 16, lanes)
        target = sink(pair)
        for q in range(half // 4 + 1):
            parts = []
            for h in range(2):
                if q < half // 4:
                    lines = mid1[h, 4 * q : 4 * q + 4].reshape(8 * side, lanes)
                    parts.append(dot_nn(yt[...], lines))
                else:
                    parts.append(dot_nn(ys[...], mid1[h, half - 1].reshape(2 * side, lanes)))
            groups = parts[0].shape[0] // 8
            joined = jnp.concatenate([p.reshape(groups, 8, lanes) for p in parts], axis=1)
            target[pl.ds(q * side, groups)] = joined.astype(BF)
        return carry

    return plane_pair, loads


def plane_kernel(side, planes, info, *refs):
    pieces = refs[:-14]
    out, *held, wann, mid1, ready, sems, out_sems = refs[-10:]
    tables = list(zip(refs[-14:-10], held))
    pairs = len(pieces) // 2 * planes

    def put(pair):
        slot = pair & 1
        return pltpu.make_async_copy(ready.at[slot], out.at[pair], out_sems.at[slot])

    plane_pair, loads = transform_planes(
        side, planes, info[1], pieces, tables, wann, mid1, sems, lambda p: ready.at[p & 1]
    )
    for load in loads:
        load.wait()

    def step(pair, carry):
        pl.when(pair >= 2)(lambda: put(pair - 2).wait())
        plane_pair(pair, carry)
        put(pair).start()
        return carry

    lax.fori_loop(0, pairs, step, 0)
    for pair in range(max(pairs - 2, 0), pairs):
        put(pair).wait()


def plane_lines(info, pieces, picks, tables, side):
    planes, members = pieces[0].shape[:2]
    half = side // 2 + 1
    lanes = 256
    pairs = len(pieces) // 2 * planes
    return pl.pallas_call(
        functools.partial(plane_kernel, side, planes),
        out_shape=jax.ShapeDtypeStruct((pairs, half * side // 4, 16, lanes), BF),
        in_specs=[pl.BlockSpec(memory_space=pltpu.SMEM)]
        + [pl.BlockSpec(memory_space=pl.ANY)] * (len(pieces) + 4),
        out_specs=pl.BlockSpec(memory_space=pl.ANY),
        scratch_shapes=[pltpu.VMEM(table.shape, BF) for table in (picks, *tables)]
        + [
            pltpu.VMEM((2 * pairs, members, side * side), F32),
            pltpu.VMEM((2, half, side // 8, 16, lanes), BF),
            pltpu.VMEM((2, half * side // 4, 16, lanes), BF),
            pltpu.SemaphoreType.DMA((len(pieces) + 4,)),
            pltpu.SemaphoreType.DMA((2,)),
        ],
        compiler_params=pltpu.CompilerParams(vmem_limit_bytes=VMEM_BYTES),
        cost_estimate=pl.CostEstimate(
            flops=600_000_000 * pairs, bytes_accessed=6_000_000, transcendentals=0
        ),
        name="plane_lines",
    )(info, *pieces, picks, *tables)


def pair_kernel(side, planes, norm, early, late, info, cells, signs, *refs):
    early_lines, pieces = refs[0], refs[1:-18]
    send, keep, *held, xt, wann, mid1, mid2, spec, stages, sems = refs[-13:]
    tables = list(zip(refs[-18:-13], held + [xt]))
    lanes = mid2.shape[-1]
    own = lanes * 3 // 4

    def place(shift, rest):
        return (info[0] ^ shift) * planes + rest

    copies = []
    for pair in range(len(early) * planes):
        to = place(early[pair // planes], pair % planes)
        copies.append(
            pltpu.make_async_copy(
                early_lines.at[pair], mid2.at[:, to], sems.at[len(pieces) + 5 + pair]
            )
        )
    plane_pair, loads = transform_planes(
        side, planes, info[1], pieces, tables[:4], wann, mid1, sems,
        lambda pair: mid2.at[:, place(late[0] + lax.div(pair, planes), pair & (planes - 1))],
    )
    copies.append(pltpu.make_async_copy(*tables[4], sems.at[len(pieces) + 4]))
    for copy in copies:
        copy.start()
    for load in loads:
        load.wait()
    lax.fori_loop(0, len(late) * planes, plane_pair, 0)
    for copy in copies:
        copy.wait()

    left = lax.broadcasted_iota(jnp.int32, (1, 128), 1) < 64

    def column(kq, carry):
        lines = dot_nn(xt[...], mid2[kq].reshape(8 * side, lanes))
        n = 4 * side
        re, im = lines[:n], lines[n:]
        thirds = (re[:, :128], im[:, :128], jnp.where(left, re[:, 128:], im[:, 128:]))
        for third in range(3):
            for odd in range(2):
                at = pl.ds(kq * 3 * n + 2 * third + odd, n // 2, stride=6)
                spec[at, :] = thirds[third][odd * n // 2 : (odd + 1) * n // 2]
        return carry

    lax.fori_loop(0, mid2.shape[0], column, 0, unroll=8)

    block = 128
    deep = stages.shape[0]

    def fill(slot, base):
        for j in range(block):
            odd, even = divmod(j, block // 2)
            row = spec[pl.ds(cells[base + j], 3, stride=2), :]
            stages[slot, pl.ds(6 * even + odd, 3, stride=2), :] = row

    def drain(slot, out, b, sign):
        at = pl.ds(pl.multiple_of(b * block, block), block)
        columns = []
        for third in range(3):
            halves = [
                stages[slot, pl.ds(2 * third + odd, block // 2, stride=6), :] for odd in range(2)
            ]
            whole = jnp.concatenate(halves, axis=0) * norm
            columns.append(jnp.transpose(whole.astype(BF)))
        half_rows = block // 2
        sign = sign.astype(BF)
        out[:block, at] = columns[0]
        out[block : block + half_rows, at] = columns[2][:half_rows]
        out[own : own + block, at] = columns[1] * sign
        out[own + block :, at] = columns[2][half_rows:] * sign

    def gather_into(out, first):
        def step(i, carry):
            for slot in range(deep):
                fill(slot, first + (i * deep + slot) * block)
            for slot in range(deep):
                b = i * deep + slot
                drain(slot, out, b, signs[pl.ds(first // block + b, 1), :])
            return carry

        lax.fori_loop(0, out.shape[1] // block // deep, step, 0)

    gather_into(send, 0)
    gather_into(keep, send.shape[1])


def pair_coefficients(
    info, cells, signs, lines, pieces, picks, tables, early, late, side, norm, send_rows
):
    keep_rows = cells.shape[0] - send_rows
    planes, members = pieces[0].shape[:2]
    half = side // 2 + 1
    lanes = 256
    pairs = side // 2
    smem = pl.BlockSpec(memory_space=pltpu.SMEM)
    vmem = pl.BlockSpec(memory_space=pltpu.VMEM)
    anywhere = pl.BlockSpec(memory_space=pl.ANY)
    return pl.pallas_call(
        functools.partial(pair_kernel, side, planes, norm, early, late),
        out_shape=(
            jax.ShapeDtypeStruct((384, send_rows), BF),
            jax.ShapeDtypeStruct((384, keep_rows), BF),
        ),
        in_specs=[smem, smem, vmem] + [anywhere] * (6 + len(pieces)),
        out_specs=(vmem, vmem),
        scratch_shapes=[pltpu.VMEM(table.shape, BF) for table in (picks, *tables)]
        + [
            pltpu.VMEM((len(pieces) * planes, members, side * side), F32),
            pltpu.VMEM((2, half, side // 8, 16, lanes), BF),
            pltpu.VMEM((half * side // 4, pairs, 16, lanes), BF),
            pltpu.VMEM((half * side * side * 3, 128), F32),
            pltpu.VMEM((4, 3 * 128, 128), F32),
            pltpu.SemaphoreType.DMA((len(pieces) + 5 + len(early) * planes,)),
        ],
        compiler_params=pltpu.CompilerParams(vmem_limit_bytes=VMEM_BYTES),
        cost_estimate=pl.CostEstimate(
            flops=20_000_000_000, bytes_accessed=25_000_000, transcendentals=0
        ),
        name="pair_coefficients",
    )(info, cells, signs, lines, *pieces, picks, *tables)


def coulomb_kernel(
    freq, shares, scale, own_first, info, keep, send, recv, w, *refs
):
    out, re, im, both, lhs, mixed, tiles, sems = refs[-8:]
    pairs, h_rows = re.shape
    g_rows = lhs.shape[1]
    tile = tiles.shape[2]
    steps = g_rows // tile
    wide, thin = pairs // 3, pairs // 6
    own = wide + thin
    cut = h_rows // CHUNKS

    def fetch(mine, columns, re_to, im_to, to_columns, base):
        copies = []
        for source, index in ((mine, info[1]), (recv, 1 - info[1])):
            for part, target in enumerate((re_to, im_to)):
                for row, to, n in (
                    (0, pl.multiple_of(index * wide, wide), wide),
                    (wide, pl.multiple_of(2 * wide + index * thin, thin), thin),
                ):
                    copies.append(
                        pltpu.make_async_copy(
                            source.at[pl.ds(part * own + row, n), columns],
                            target.at[pl.ds(to, n), to_columns],
                            sems.at[base + len(copies)],
                        )
                    )
        return copies

    def tile_copy(step, columns, slot, sem):
        rows = pl.ds(pl.multiple_of(step * tile, tile), tile)
        return pltpu.make_async_copy(
            w.at[freq, :, rows, columns], tiles.at[slot, :, :, columns], sems.at[sem]
        )

    whole = pl.ds(0, h_rows)
    spans = [pl.ds(k * cut, cut) for k in range(CHUNKS)]
    first = [
        fetch(keep, span, re, im, span, 10 * k) + [tile_copy(0, span, 0, 10 * k + 8)]
        for k, span in enumerate(spans)
    ]
    left = fetch(
        send,
        pl.ds(h_rows, g_rows),
        lhs.at[pl.ds(0, pairs)],
        lhs.at[pl.ds(pairs, pairs)],
        pl.ds(0, g_rows),
        10 * CHUNKS,
    )
    later = 10 * CHUNKS + 8

    for copies in first:
        for copy in copies:
            copy.start()
    tile_copy(1, whole, 1, later + 1).start()
    for copy in left:
        copy.start()

    def products(slot, columns):
        w_re, w_im = tiles[slot, 0, :, columns], tiles[slot, 1, :, columns]
        w_both = (w_re.astype(F32) + w_im.astype(F32)).astype(BF)
        return (
            dot_nt(re[:, columns], w_re),
            dot_nt(im[:, columns], w_im),
            dot_nt(both[:, columns], w_both),
        )

    def mix(step, re_re, im_im, all_all):
        at = pl.ds(pl.multiple_of(step * tile, tile), tile)
        mixed[:pairs, at] = (re_re - im_im).astype(BF)
        mixed[pairs:, at] = (all_all - re_re - im_im).astype(BF)

    total = None
    for span, copies in zip(spans, first):
        for copy in copies:
            copy.wait()
        both[:, span] = (re[:, span].astype(F32) + im[:, span].astype(F32)).astype(BF)
        terms = products(0, span)
        total = terms if total is None else tuple(a + b for a, b in zip(total, terms))
    mix(0, *total)

    def further(step, carry):
        slot = step & 1

        @pl.when(step + 1 < steps)
        def _():
            tile_copy(step + 1, whole, 1 - slot, later + 1 - slot).start()

        tile_copy(step, whole, slot, later + slot).wait()
        mix(step, *products(slot, whole))
        return carry

    lax.fori_loop(1, steps, further, 0)

    for copy in left:
        copy.wait()
    terms = dot_nt(lhs[...], mixed[...])
    u = (
        (terms[:pairs, :pairs] + terms[pairs:, pairs:]) * scale,
        (terms[:pairs, pairs:] - terms[pairs:, :pairs]) * scale,
    )
    n = pairs // shares
    for part in range(2):
        for s in range(shares):
            to = (s % 2 ^ info[1]) * (shares // 2) + s // 2 if own_first else s
            out[to, part] = u[part][s * n : (s + 1) * n].astype(BF)


def coulomb_partial(info, keep, send, recv, screened, freq, shares, scale, own_first, after):
    _, _, g_rows, h_rows = screened.shape
    pairs = keep.shape[0]
    tile = min(256, g_rows // 2)
    anywhere = pl.BlockSpec(memory_space=pl.ANY)
    return pl.pallas_call(
        functools.partial(coulomb_kernel, freq, shares, scale, own_first),
        out_shape=jax.ShapeDtypeStruct((shares, 2, pairs // shares, pairs), BF),
        in_specs=[pl.BlockSpec(memory_space=pltpu.SMEM)] + [anywhere] * (4 + len(after)),
        out_specs=pl.BlockSpec(memory_space=pltpu.VMEM),
        scratch_shapes=[
            pltpu.VMEM((pairs, h_rows), BF),
            pltpu.VMEM((pairs, h_rows), BF),
            pltpu.VMEM((pairs, h_rows), BF),
            pltpu.VMEM((2 * pairs, g_rows), BF),
            pltpu.VMEM((2 * pairs, g_rows), BF),
            pltpu.VMEM((2, 2, tile, h_rows), BF),
            pltpu.SemaphoreType.DMA((10 * CHUNKS + 10,)),
        ],
        compiler_params=pltpu.CompilerParams(vmem_limit_bytes=VMEM_BYTES),
        cost_estimate=pl.CostEstimate(
            flops=14_000_000_000, bytes_accessed=25_000_000, transcendentals=0
        ),
        name="coulomb_partial",
    )(info, keep, send, recv, screened, *after)


def cell_table(gmap, side):
    kx, ky, kz = gmap // (side * side), gmap // side % side, gmap % side
    mirrored = kz > side // 2
    kx, ky, kz = (jnp.where(mirrored, -k % side, k) for k in (kx, ky, kz))
    place = kx * 4 + ky % 4
    cells = (kz * (side // 4) + ky // 4) * 12 * side + place % (2 * side) * 6 + place // (2 * side)
    return cells, jnp.where(mirrored, -1.0, 1.0).astype(F32)


def shards(rows, cols, wannier, pairs, gmap, screened):
    members, _, grid_cells = wannier.shape
    side = math.isqrt(grid_cells)
    count = pairs.shape[0]
    waves = gmap.shape[0]
    g_rows, h_rows = screened.shape[2:]
    row, col = lax.axis_index("row"), lax.axis_index("col")
    info = jnp.stack([row, col]).astype(jnp.int32)
    swap = [(0, 1), (1, 0)]

    local = wannier.transpose(1, 0, 2)
    same = {0: local}
    for bit in reversed(range(log2(rows))):
        hop = [(i, i ^ (1 << bit)) for i in range(rows)]
        for shift in list(same):
            same[shift ^ (1 << bit)] = lax.ppermute(same[shift], "row", hop)
    cross = {}
    for shift in range(rows):
        cross[shift] = lax.ppermute(same[shift], "col", swap)

    wide = count // 3
    first = lax.dynamic_slice_in_dim(pairs, col * wide, wide, 0)
    last = lax.dynamic_slice_in_dim(pairs, 2 * wide + col * (wide // 2), wide // 2, 0)
    owned = jnp.concatenate([first, last], axis=0).T.reshape(-1, 1)
    picks = (owned == jnp.arange(2 * members, dtype=jnp.int32)[None, :] % members).astype(BF)

    norm = 1.0 / (math.sqrt(side**3) * SCALE**3)
    cells, signs = cell_table(gmap, side)

    def arranged(table):
        theirs = lax.dynamic_slice_in_dim(table, (1 - col) * h_rows, h_rows)
        block = lax.dynamic_slice_in_dim(table, row * g_rows, g_rows)
        ours = lax.dynamic_slice_in_dim(table, col * h_rows, h_rows)
        return jnp.concatenate([theirs, block, ours])

    cells, signs = arranged(cells), arranged(signs).reshape(-1, 128)
    info, cells, signs, picks = lax.optimization_barrier((info, cells, signs, picks))
    tables = stage_tables(side)
    early, late = tuple(range(rows // 2)), tuple(range(rows // 2, rows))

    def pieces(group):
        return [same[i] for i in group] + [cross[i] for i in group]

    lines = plane_lines(info, pieces(early), picks, tables[:3], side)
    send, keep = pair_coefficients(
        info, cells, signs, lines, pieces(late), picks, tables, early, late,
        side, norm, h_rows + g_rows,
    )
    recv = lax.ppermute(send, "col", swap)
    results, after = [], ()
    freqs = screened.shape[0]
    for freq in range(freqs):
        last = freq == freqs - 1
        partial = coulomb_partial(
            info, keep, send, recv, screened, freq, rows * cols, 1.0 / math.sqrt(waves), last, after
        )
        after = (partial,)
        axes = ("row", "col")
        if last:
            chip = partial[:rows].astype(F32) + lax.ppermute(partial[rows:], "col", swap)
            partial, axes = chip.astype(BF), "row"
        if results:
            partial, results[-1] = lax.optimization_barrier((partial, results[-1]))
        spread = lax.all_to_all(partial, axes, split_axis=0, concat_axis=0, tiled=True)
        results.append(jnp.sum(spread.astype(F32), axis=0))
    return jnp.stack(results)


def solution(mesh):
    rows, cols = mesh.shape["row"], mesh.shape["col"]

    def body(*arrays):
        return shards(rows, cols, *arrays)

    return jax.shard_map(
        body,
        mesh=mesh,
        in_specs=(P("kpt", ("row", "col"), None), P(), P(), P("kpt", None, "row", "col")),
        out_specs=P(None, None, ("kpt", "row", "col"), None),
        check_vma=False,
    )
```

time: 169 us -> 161 us (0.953)
  blocking collectives: 22.5 us -> 16.3 us
  starting transfers between devices: 12.9 us -> 18.8 us
  waiting for transfers between devices: 31.1 us -> 26.3 us
  Pallas kernels: 91.3 us -> 87.7 us
    all_to_all x1, blocking collectives: 22.5 us -> 16.3 us  [shards(): lax.all_to_all(partial, axes, split_axis=0, concat_axis=0, tiled=True)]
    all_to_all x0 -> x1, starting transfers between devices: none -> 5.52 us  [shards(): lax.all_to_all(partial, axes, split_axis=0, concat_axis=0, tiled=True)]
    ppermute x16, waiting for transfers between devices: 24.3 us -> 19.5 us  [the longest x7 18.3 us: shards(): same[shift ^ 1 << bit] = lax.ppermute(same[shift], 'row', hop)]
    pallas_call x2 -> x4, Pallas kernels: 91.3 us -> 87.7 us  [the longest x1 37.7 us: pair_coefficients(): pl.pallas_call(functools.partial(pair_kernel, side, planes, norm, early,...]
  transfers between devices with their start and end apart: 17 -> 18, of which waited for: 7 -> 8; matrix products, arithmetic and copies ran while one was open for 3% -> 5% of each run, Pallas kernels for 0% -> 20%
where the time goes in v3:
time: 161 us; the launch traced here: 160 us
  Pallas kernels  87.7 us (54%)
  waiting for transfers between devices  26.3 us (16%)
  starting transfers between devices  18.8 us (12%)
  blocking collectives  16.3 us (10%)
  other arithmetic  7.2 us (4%)
  local copies, waits for them, and re-layouts  3.62 us (2%)
    pallas_call x1, Pallas kernels, pair_coefficients(): pl.pallas_call(functools.partial(pair_kernel, side, planes, norm, early,...  37.7 us
    pallas_call x2, Pallas kernels, coulomb_partial(): pl.pallas_call(functools.partial(coulomb_kernel, freq, shares, scale, own...  35.1 us
    ppermute x7, waiting for transfers between devices, shards(): same[shift ^ 1 << bit] = lax.ppermute(same[shift], 'row', hop)  18.3 us
    all_to_all x1, blocking collectives, shards(): lax.all_to_all(partial, axes, split_axis=0, concat_axis=0, tiled=True)  16.3 us
    pallas_call x1, Pallas kernels, plane_lines(): pl.pallas_call(functools.partial(plane_kernel, side, planes), out_shape=j...  14.9 us
    ppermute x7, starting transfers between devices, shards(): same[shift ^ 1 << bit] = lax.ppermute(same[shift], 'row', hop)  11.1 us
    ppermute x1, waiting for transfers between devices, shards(): recv = lax.ppermute(send, 'col', swap)  6.75 us
    all_to_all x1, starting transfers between devices, shards(): lax.all_to_all(partial, axes, split_axis=0, concat_axis=0, tiled=True)  5.52 us
  transfers between devices with their start and end apart: 18, of which 8 were waited for; matrix products, arithmetic and copies ran while one was open for 5% of the time, Pallas kernels for 20%

profile of v3, /device:TPU:0, one launch (start us, length us, event | category | flops | bytes accessed | tf_op | source)
XLA Modules:
  0.0 160.0 jit_solution(9977442964544633898)
XLA Ops:
  0.0 1.0 copy.11
  1.0 4.1 %collective-permute-start.7 = (f32[2,32,1024]{2,1,0:T(8,128)S(1)}, f32[2,32,1024]{2,1,0:T(8,128)}, u32[]{:S(2)}, u32[]{:S(2)}) collective-permute-start(f32[2,32,1024]{2,1,0:T(8,128)S(1)} %bitcast.13), channel_id=1, source_target_pairs={{0,8},{2,10},{4,12},{6,14},{8,0},{10,2},{12,4},{14,6},{1,9},{3,11}... | collective-permute-start | bytes 786440 | tf_op jit(solution)/shard_map/ppermute | solution.py:446
  5.2 0.0 collective-permute-start.3
  5.2 1.6 collective-permute-start.1
  6.8 1.5 collective-permute-start
  8.3 0.9 fusion.8
  9.2 0.8 compare_select_fusion
  10.0 0.8 constant_dynamic-slice_fusion
  10.7 0.7 constant_dynamic-slice_fusion.1
  11.5 0.6 maximum_bitcast_fusion.signs
  12.1 5.2 %collective-permute-done.7.refs_1_ = f32[2,32,1024]{2,1,0:T(8,128)} collective-permute-done((f32[2,32,1024]{2,1,0:T(8,128)S(1)}, f32[2,32,1024]{2,1,0:T(8,128)}, u32[]{:S(2)}, u32[]{:S(2)}) %collective-permute-start.7) | collective-permute-done | bytes 262176 | tf_op jit(solution)/shard_map/ppermute | solution.py:446
  17.3 0.6 collective-permute-start.9
  17.9 0.5 collective-permute-done.1.refs_2_
  18.4 1.6 collective-permute-start.2
  19.9 0.6 pad_add_fusion.cells
  20.6 0.5 collective-permute-start.8
  21.0 0.0 collective-permute-start.5
  21.0 0.0 collective-permute-done.refs_1_
  21.0 0.5 collective-permute-start.4
  21.5 3.5 %collective-permute-done.9.refs_3_ = f32[2,32,1024]{2,1,0:T(8,128)} collective-permute-done((f32[2,32,1024]{2,1,0:T(8,128)}, f32[2,32,1024]{2,1,0:T(8,128)}, u32[]{:S(2)}, u32[]{:S(2)}) %collective-permute-start.9) | collective-permute-done | bytes 262176 | tf_op jit(solution)/shard_map/ppermute | solution.py:446
  25.0 1.3 collective-permute-start.10
  26.4 1.2 collective-permute-done.2.refs_3_
  27.5 0.0 collective-permute-start.6
  27.5 0.6 pad_add_fusion.1.info
  28.1 0.1 eq.25
  28.2 0.8 compare_convert_fusion.refs_8_.refs_9_
  29.0 4.3 %collective-permute-done.8.refs_2_ = f32[2,32,1024]{2,1,0:T(8,128)} collective-permute-done((f32[2,32,1024]{2,1,0:T(8,128)}, f32[2,32,1024]{2,1,0:T(8,128)}, u32[]{:S(2)}, u32[]{:S(2)}) %collective-permute-start.8) | collective-permute-done | bytes 262176 | tf_op jit(solution)/shard_map/ppermute | solution.py:446
  33.3 0.0 collective-permute-start.11
  33.3 0.0 collective-permute-done.5.refs_6_
  33.3 0.6 collective-permute-start.13
  33.8 0.0 collective-permute-done.4.refs_5_
  33.8 0.1 collective-permute-start.12
  34.0 0.0 copy-done.5
  34.0 3.6 %collective-permute-done.10.refs_4_ = f32[2,32,1024]{2,1,0:T(8,128)} collective-permute-done((f32[2,32,1024]{2,1,0:T(8,128)}, f32[2,32,1024]{2,1,0:T(8,128)}, u32[]{:S(2)}, u32[]{:S(2)}) %collective-permute-start.10) | collective-permute-done | bytes 262176 | tf_op jit(solution)/shard_map/ppermute | solution.py:446
  37.6 14.9 %plane_lines.1.refs_0_ = bf16[8,136,16,256]{3,2,1,0:T(8,128)(2,1)} custom-call(s32[2]{0:T(128)} %pad_add_fusion.1.info, f32[2,32,1024]{2,1,0:T(8,128)} %bitcast.17, f32[2,32,1024]{2,1,0:T(8,128)} %copy-done.3, f32[2,32,1024]{2,1,0:T(8,128)} %copy-done.2, f32[2,32,1024]{2,1,0:T(8,128)} %copy-done.4, f32[2,32,1024]{2,1,0:T(8,128)} %copy-done.1, ...), custom_call_target="tpu_custom_call" | custom-call | flops 4800000000 | bytes 6000000 | tf_op jit(solution)/shard_map/plane_lines/pallas_call | solution.py:143
  52.5 37.7 %pair_coefficients.1 = (bf16[384,5120]{1,0:T(8,128)(2,1)}, bf16[384,4096]{1,0:T(8,128)(2,1)}) custom-call(s32[2]{0:T(128)} %pad_add_fusion.1.info, s32[9216]{0:T(1024)} %pad_add_fusion.cells, f32[72,128]{1,0:T(8,128)} %maximum_bitcast_fusion.signs, bf16[8,136,16,256]{3,2,1,0:T(8,128)(2,1)} %plane_lines.1.refs_0_, ...), custom_call_target="tpu_custom_call" | custom-call | flops 20000000000 | bytes 25000000 | tf_op jit(solution)/shard_map/pair_coefficients/pallas_call | solution.py:262
  90.2 0.6 collective-permute-start.15
  90.8 6.8 %collective-permute-done.15.recv = bf16[384,5120]{1,0:T(8,128)(2,1)} collective-permute-done((bf16[384,5120]{1,0:T(8,128)(2,1)}, bf16[384,5120]{1,0:T(8,128)(2,1)}, u32[]{:S(2)}, u32[]{:S(2)}) %collective-permute-start.15) | collective-permute-done | bytes 3932192 | tf_op jit(solution)/shard_map/ppermute | solution.py:479
  97.6 17.5 %coulomb_partial.2.refs_0_ = bf16[16,2,24,384]{3,2,1,0:T(8,128)(2,1)} custom-call(s32[2]{0:T(128)} %pad_add_fusion.1.info, bf16[384,4096]{1,0:T(8,128)(2,1)} %get-tuple-element.17.keep, bf16[384,5120]{1,0:T(8,128)(2,1)} %get-tuple-element.18.send, bf16[384,5120]{1,0:T(8,128)(2,1)} %collective-permute-done.15.recv, bf16[2,2,1024,4096]{3,2,1,0:T(8,128)(2,1)} %w.3), custom_call_target="tpu_custom_call" | custom-call | flops 14000000000 | bytes 25000000 | tf_op jit(solution)/shard_map/coulomb_partial/pallas_call | solution.py:400
  115.1 5.5 %all-to-all-start = ((bf16[16,2,24,384]{3,2,1,0:T(8,128)(2,1)}), bf16[16,2,24,384]{3,2,1,0:T(8,128)(2,1)}, u32[]{:S(2)}, u32[]{:S(2)}) async-start(bf16[16,2,24,384]{3,2,1,0:T(8,128)(2,1)} %coulomb_partial.2.refs_0_), calls=%async_computation | async-start | bytes 1179648 | tf_op jit(solution)/shard_map/all_to_all | solution.py:494
  120.6 17.6 %coulomb_partial.3 = bf16[16,2,24,384]{3,2,1,0:T(8,128)(2,1)} custom-call(s32[2]{0:T(128)} %pad_add_fusion.1.info, bf16[384,4096]{1,0:T(8,128)(2,1)} %get-tuple-element.17.keep, bf16[384,5120]{1,0:T(8,128)(2,1)} %get-tuple-element.18.send, bf16[384,5120]{1,0:T(8,128)(2,1)} %collective-permute-done.15.recv, bf16[2,2,1024,4096]{3,2,1,0:T(8,128)(2,1)} %w.3, ...), custom_call_target="tpu_custom_call" | custom-call | flops 14000000000 | bytes 25000000 | tf_op jit(solution)/shard_map/coulomb_partial/pallas_call | solution.py:400
  138.2 1.0 slice.9
  139.2 0.4 collective-permute-start.16
  139.6 1.2 collective-permute-done.16
  140.8 1.0 add_convert_fusion
  141.9 1.2 convert_reduce_fusion
  143.0 16.3 %all_to_all.10 = bf16[8,2,24,384]{3,2,1,0:T(8,128)(2,1)S(1)} all-to-all(bf16[8,2,24,384]{3,2,1,0:T(8,128)(2,1)S(1)} %add_convert_fusion), channel_id=1, replica_groups=mesh['kpt'=2,'row'=8,'col'=2] {'row'}, dimensions={0} | all-to-all | bytes 589824 | tf_op jit(solution)/shard_map/all_to_all | solution.py:494
  159.4 0.7 pad_maximum_fusion
  (28 shorter events, 0.1 us)
Async XLA Ops:
  1.0 5.7 %copy-start = (f32[32,2,1024]{2,0,1:T(8,128)}, f32[32,2,1024]{2,0,1:T(8,128)S(1)}, u32[]{:S(2)}) copy-start(f32[32,2,1024]{2,0,1:T(8,128)S(1)} %copy.11) | copy-start | bytes 786436
  1.0 16.3 %collective-permute-start.7 = (f32[2,32,1024]{2,1,0:T(8,128)S(1)}, f32[2,32,1024]{2,1,0:T(8,128)}, u32[]{:S(2)}, u32[]{:S(2)}) collective-permute-start(f32[2,32,1024]{2,1,0:T(8,128)S(1)} %bitcast.13), channel_id=1, source_target_pairs={{0,8},{2,10},{4,12},{6,14},{8,0},{10,2},{12,4},{14,6},{1,9},{3,11}... | collective-permute-start | bytes 786440 | tf_op jit(solution)/shard_map/ppermute | solution.py:446
  5.2 15.8 %collective-permute-start.3 = (f32[2,32,1024]{2,1,0:T(8,128)S(1)}, f32[2,32,1024]{2,1,0:T(8,128)S(1)}, u32[]{:S(2)}, u32[]{:S(2)}) collective-permute-start(f32[2,32,1024]{2,1,0:T(8,128)S(1)} %bitcast.14), channel_id=1, source_target_pairs={{0,1},{1,0},{2,3},{3,2},{4,5},{5,4},{6,7},{7,6},{8,9},{9,8},{10,11... | collective-permute-start | bytes 786440 | tf_op jit(solution)/shard_map/ppermute | solution.py:449
  5.2 13.2 %collective-permute-start.1 = (f32[2,32,1024]{2,1,0:T(8,128)S(1)}, f32[2,32,1024]{2,1,0:T(8,128)S(1)}, u32[]{:S(2)}, u32[]{:S(2)}) collective-permute-start(f32[2,32,1024]{2,1,0:T(8,128)S(1)} %bitcast.15), channel_id=1, source_target_pairs={{0,4},{2,6},{4,0},{6,2},{8,12},{10,14},{12,8},{14,10},{1,5},{3,7},... | collective-permute-start | bytes 786440 | tf_op jit(solution)/shard_map/ppermute | solution.py:446
  6.8 14.3 %collective-permute-start = (f32[2,32,1024]{2,1,0:T(8,128)S(1)}, f32[2,32,1024]{2,1,0:T(8,128)S(1)}, u32[]{:S(2)}, u32[]{:S(2)}) collective-permute-start(f32[2,32,1024]{2,1,0:T(8,128)S(1)} %bitcast.16), channel_id=1, source_target_pairs={{0,2},{2,0},{4,6},{6,4},{8,10},{10,8},{12,14},{14,12},{1,3},{3,1},... | collective-permute-start | bytes 786440 | tf_op jit(solution)/shard_map/ppermute | solution.py:446
  17.3 7.7 %collective-permute-start.9 = (f32[2,32,1024]{2,1,0:T(8,128)}, f32[2,32,1024]{2,1,0:T(8,128)}, u32[]{:S(2)}, u32[]{:S(2)}) collective-permute-start(f32[2,32,1024]{2,1,0:T(8,128)} %collective-permute-done.7.refs_1_), channel_id=1, source_target_pairs={{0,4},{2,6},{4,0},{6,2},{8,12},{10,14},{12,8},{14,10},{1,5},{3,7},... | collective-permute-start | bytes 786440 | tf_op jit(solution)/shard_map/ppermute | solution.py:446
  18.4 14.9 %copy-start.2 = (f32[2,32,1024]{2,1,0:T(8,128)}, f32[2,32,1024]{2,1,0:T(8,128)S(1)}, u32[]{:S(2)}) copy-start(f32[2,32,1024]{2,1,0:T(8,128)S(1)} %collective-permute-done.1.refs_2_) | copy-start | bytes 786436
  18.4 9.2 %collective-permute-start.2 = (f32[2,32,1024]{2,1,0:T(8,128)S(1)}, f32[2,32,1024]{2,1,0:T(8,128)S(1)}, u32[]{:S(2)}, u32[]{:S(2)}) collective-permute-start(f32[2,32,1024]{2,1,0:T(8,128)S(1)} %collective-permute-done.1.refs_2_), channel_id=1, source_target_pairs={{0,2},{2,0},{4,6},{6,4},{8,10},{10,8},{12,14},{14,12},{1,3},{3,1},... | collective-permute-start | bytes 786440 | tf_op jit(solution)/shard_map/ppermute | solution.py:446
  20.6 12.7 %collective-permute-start.8 = (f32[2,32,1024]{2,1,0:T(8,128)}, f32[2,32,1024]{2,1,0:T(8,128)}, u32[]{:S(2)}, u32[]{:S(2)}) collective-permute-start(f32[2,32,1024]{2,1,0:T(8,128)} %collective-permute-done.7.refs_1_), channel_id=1, source_target_pairs={{0,2},{2,0},{4,6},{6,4},{8,10},{10,8},{12,14},{14,12},{1,3},{3,1},... | collective-permute-start | bytes 786440 | tf_op jit(solution)/shard_map/ppermute | solution.py:446
  21.0 8.0 %copy-start.1 = (f32[2,32,1024]{2,1,0:T(8,128)}, f32[2,32,1024]{2,1,0:T(8,128)S(1)}, u32[]{:S(2)}) copy-start(f32[2,32,1024]{2,1,0:T(8,128)S(1)} %collective-permute-done.3.refs_4_) | copy-start | bytes 786436
  21.0 12.3 %collective-permute-start.5 = (f32[2,32,1024]{2,1,0:T(8,128)S(1)}, f32[2,32,1024]{2,1,0:T(8,128)S(1)}, u32[]{:S(2)}, u32[]{:S(2)}) collective-permute-start(f32[2,32,1024]{2,1,0:T(8,128)S(1)} %collective-permute-done.1.refs_2_), channel_id=1, source_target_pairs={{0,1},{1,0},{2,3},{3,2},{4,5},{5,4},{6,7},{7,6},{8,9},{9,8},{10,11... | collective-permute-start | bytes 786440 | tf_op jit(solution)/shard_map/ppermute | solution.py:449
  21.0 12.2 %copy-start.3 = (f32[2,32,1024]{2,1,0:T(8,128)}, f32[2,32,1024]{2,1,0:T(8,128)S(1)}, u32[]{:S(2)}) copy-start(f32[2,32,1024]{2,1,0:T(8,128)S(1)} %collective-permute-done.refs_1_) | copy-start | bytes 786436
  21.0 12.8 %collective-permute-start.4 = (f32[2,32,1024]{2,1,0:T(8,128)S(1)}, f32[2,32,1024]{2,1,0:T(8,128)S(1)}, u32[]{:S(2)}, u32[]{:S(2)}) collective-permute-start(f32[2,32,1024]{2,1,0:T(8,128)S(1)} %collective-permute-done.refs_1_), channel_id=1, source_target_pairs={{0,1},{1,0},{2,3},{3,2},{4,5},{5,4},{6,7},{7,6},{8,9},{9,8},{10,11... | collective-permute-start | bytes 786440 | tf_op jit(solution)/shard_map/ppermute | solution.py:449
  25.0 12.5 %collective-permute-start.10 = (f32[2,32,1024]{2,1,0:T(8,128)}, f32[2,32,1024]{2,1,0:T(8,128)}, u32[]{:S(2)}, u32[]{:S(2)}) collective-permute-start(f32[2,32,1024]{2,1,0:T(8,128)} %collective-permute-done.9.refs_3_), channel_id=1, source_target_pairs={{0,2},{2,0},{4,6},{6,4},{8,10},{10,8},{12,14},{14,12},{1,3},{3,1},... | collective-permute-start | bytes 786440 | tf_op jit(solution)/shard_map/ppermute | solution.py:446
  27.5 6.3 %copy-start.4 = (f32[2,32,1024]{2,1,0:T(8,128)}, f32[2,32,1024]{2,1,0:T(8,128)S(1)}, u32[]{:S(2)}) copy-start(f32[2,32,1024]{2,1,0:T(8,128)S(1)} %collective-permute-done.2.refs_3_) | copy-start | bytes 786436
  27.5 10.0 %collective-permute-start.6 = (f32[2,32,1024]{2,1,0:T(8,128)S(1)}, f32[2,32,1024]{2,1,0:T(8,128)}, u32[]{:S(2)}, u32[]{:S(2)}) collective-permute-start(f32[2,32,1024]{2,1,0:T(8,128)S(1)} %collective-permute-done.2.refs_3_), channel_id=1, source_target_pairs={{0,1},{1,0},{2,3},{3,2},{4,5},{5,4},{6,7},{7,6},{8,9},{9,8},{10,11... | collective-permute-start | bytes 786440 | tf_op jit(solution)/shard_map/ppermute | solution.py:449
  33.3 19.2 %collective-permute-start.11 = (f32[2,32,1024]{2,1,0:T(8,128)}, f32[2,32,1024]{2,1,0:T(8,128)}, u32[]{:S(2)}, u32[]{:S(2)}) collective-permute-start(f32[2,32,1024]{2,1,0:T(8,128)} %collective-permute-done.7.refs_1_), channel_id=1, source_target_pairs={{0,1},{1,0},{2,3},{3,2},{4,5},{5,4},{6,7},{7,6},{8,9},{9,8},{10,11... | collective-permute-start | bytes 786440 | tf_op jit(solution)/shard_map/ppermute | solution.py:449
  33.3 0.7 copy-start.5
  33.3 19.2 %collective-permute-start.13 = (f32[2,32,1024]{2,1,0:T(8,128)}, f32[2,32,1024]{2,1,0:T(8,128)}, u32[]{:S(2)}, u32[]{:S(2)}) collective-permute-start(f32[2,32,1024]{2,1,0:T(8,128)} %collective-permute-done.9.refs_3_), channel_id=1, source_target_pairs={{0,1},{1,0},{2,3},{3,2},{4,5},{5,4},{6,7},{7,6},{8,9},{9,8},{10,11... | collective-permute-start | bytes 786440 | tf_op jit(solution)/shard_map/ppermute | solution.py:449
  33.8 3.7 %copy-start.6 = (f32[2,32,1024]{2,1,0:T(8,128)}, f32[2,32,1024]{2,1,0:T(8,128)S(1)}, u32[]{:S(2)}) copy-start(f32[2,32,1024]{2,1,0:T(8,128)S(1)} %collective-permute-done.4.refs_5_) | copy-start | bytes 786436
  33.8 18.6 %collective-permute-start.12 = (f32[2,32,1024]{2,1,0:T(8,128)}, f32[2,32,1024]{2,1,0:T(8,128)}, u32[]{:S(2)}, u32[]{:S(2)}) collective-permute-start(f32[2,32,1024]{2,1,0:T(8,128)} %collective-permute-done.8.refs_2_), channel_id=1, source_target_pairs={{0,1},{1,0},{2,3},{3,2},{4,5},{5,4},{6,7},{7,6},{8,9},{9,8},{10,11... | collective-permute-start | bytes 786440 | tf_op jit(solution)/shard_map/ppermute | solution.py:449
  37.6 14.9 %collective-permute-start.14 = (f32[2,32,1024]{2,1,0:T(8,128)}, f32[2,32,1024]{2,1,0:T(8,128)}, u32[]{:S(2)}, u32[]{:S(2)}) collective-permute-start(f32[2,32,1024]{2,1,0:T(8,128)} %collective-permute-done.10.refs_4_), channel_id=1, source_target_pairs={{0,1},{1,0},{2,3},{3,2},{4,5},{5,4},{6,7},{7,6},{8,9},{9,8},{10,11... | collective-permute-start | bytes 786440 | tf_op jit(solution)/shard_map/ppermute | solution.py:449
  90.2 7.3 %collective-permute-start.15 = (bf16[384,5120]{1,0:T(8,128)(2,1)}, bf16[384,5120]{1,0:T(8,128)(2,1)}, u32[]{:S(2)}, u32[]{:S(2)}) collective-permute-start(bf16[384,5120]{1,0:T(8,128)(2,1)} %get-tuple-element.18.send), channel_id=1, source_target_pairs={{0,1},{1,0},{2,3},{3,2},{4,5},{5,4},{6,7},{7,6},{8,9},{9,8},{10,11... | collective-permute-start | bytes 11796488 | tf_op jit(solution)/shard_map/ppermute | solution.py:479
  115.1 26.8 %all-to-all-start = ((bf16[16,2,24,384]{3,2,1,0:T(8,128)(2,1)}), bf16[16,2,24,384]{3,2,1,0:T(8,128)(2,1)}, u32[]{:S(2)}, u32[]{:S(2)}) async-start(bf16[16,2,24,384]{3,2,1,0:T(8,128)(2,1)} %coulomb_partial.2.refs_0_), calls=%async_computation | async-start | bytes 1179648 | tf_op jit(solution)/shard_map/all_to_all | solution.py:494
  139.2 1.6 %collective-permute-start.16 = (bf16[8,2,24,384]{3,2,1,0:T(8,128)(2,1)S(1)}, bf16[8,2,24,384]{3,2,1,0:T(8,128)(2,1)S(1)}, u32[]{:S(2)}, u32[]{:S(2)}) collective-permute-start(bf16[8,2,24,384]{3,2,1,0:T(8,128)(2,1)S(1)} %slice.9), channel_id=1, source_target_pairs={{0,1},{1,0},{2,3},{3,2},{4,5},{5,4},{6,7},{7,6},{8,9},{9,8},{10,11... | collective-permute-start | bytes 884744 | tf_op jit(solution)/shard_map/ppermute | solution.py:490

commit v4 on v3

--- a/solution.py
+++ b/solution.py
@@ -163,9 +163,9 @@
 
 
 def pair_kernel(side, planes, norm, early, late, info, cells, signs, *refs):
-    early_lines, pieces = refs[0], refs[1:-18]
-    send, keep, *held, xt, wann, mid1, mid2, spec, stages, sems = refs[-13:]
-    tables = list(zip(refs[-18:-13], held + [xt]))
+    early_lines, pieces = refs[0], refs[1:-21]
+    send, keep, *held, xt, sent, kept, wann, mid1, mid2, spec, stages, sems, out_sems = refs[-16:]
+    tables = list(zip(refs[-21:-16], held + [xt]))
     lanes = mid2.shape[-1]
     own = lanes * 3 // 4
 
@@ -233,19 +233,30 @@
         out[own : own + block, at] = columns[1] * sign
         out[own + block :, at] = columns[2][half_rows:] * sign
 
-    def gather_into(out, first):
+    def gather_into(held, out, first, base):
+        width = deep * block
+
+        def put(i):
+            at = pl.ds(pl.multiple_of(i * width, width), width)
+            return pltpu.make_async_copy(held.at[:, at], out.at[:, at], out_sems.at[base + i])
+
         def step(i, carry):
             for slot in range(deep):
                 fill(slot, first + (i * deep + slot) * block)
             for slot in range(deep):
                 b = i * deep + slot
-                drain(slot, out, b, signs[pl.ds(first // block + b, 1), :])
+                drain(slot, held, b, signs[pl.ds(first // block + b, 1), :])
+            put(i).start()
             return carry
 
-        lax.fori_loop(0, out.shape[1] // block // deep, step, 0)
-
-    gather_into(send, 0)
-    gather_into(keep, send.shape[1])
+        steps = out.shape[1] // width
+        lax.fori_loop(0, steps, step, 0)
+        return [functools.partial(put, i) for i in range(steps)]
+
+    puts = gather_into(sent, send, 0, 0)
+    puts += gather_into(kept, keep, send.shape[1], len(puts))
+    for put in puts:
+        put().wait()
 
 
 def pair_coefficients(
@@ -266,15 +277,18 @@
             jax.ShapeDtypeStruct((384, keep_rows), BF),
         ),
         in_specs=[smem, smem, vmem] + [anywhere] * (6 + len(pieces)),
-        out_specs=(vmem, vmem),
+        out_specs=(anywhere, anywhere),
         scratch_shapes=[pltpu.VMEM(table.shape, BF) for table in (picks, *tables)]
         + [
+            pltpu.VMEM((384, send_rows), BF),
+            pltpu.VMEM((384, keep_rows), BF),
             pltpu.VMEM((len(pieces) * planes, members, side * side), F32),
             pltpu.VMEM((2, half, side // 8, 16, lanes), BF),
             pltpu.VMEM((half * side // 4, pairs, 16, lanes), BF),
             pltpu.VMEM((half * side * side * 3, 128), F32),
             pltpu.VMEM((4, 3 * 128, 128), F32),
             pltpu.SemaphoreType.DMA((len(pieces) + 5 + len(early) * planes,)),
+            pltpu.SemaphoreType.DMA(((send_rows + keep_rows) // 512,)),
         ],
         compiler_params=pltpu.CompilerParams(vmem_limit_bytes=VMEM_BYTES),
         cost_estimate=pl.CostEstimate(
@@ -487,7 +501,7 @@
         after = (partial,)
         axes = ("row", "col")
         if last:
-            chip = partial[:rows].astype(F32) + lax.ppermute(partial[rows:], "col", swap)
+            chip = partial[:rows].astype(F32) + lax.ppermute(partial, "col", swap)[rows:]
             partial, axes = chip.astype(BF), "row"
         if results:
             partial, results[-1] = lax.optimization_barrier((partial, results[-1]))

time: 161 us -> 158 us (0.981)
  Pallas kernels: 87.7 us -> 85.8 us
    pallas_call x1, Pallas kernels: 37.7 us -> 35.8 us  [pair_coefficients(): pl.pallas_call(functools.partial(pair_kernel, side, planes, norm, early,...]
  transfers between devices with their start and end apart: 18 -> 18, of which waited for: 8 -> 8; matrix products, arithmetic and copies ran while one was open for 5% -> 4% of each run, Pallas kernels for 20% -> 21%
where the time goes in v4:
time: 158 us
  Pallas kernels  85.8 us (54%)
  waiting for transfers between devices  26.9 us (17%)
  starting transfers between devices  18.8 us (12%)
  blocking collectives  16.3 us (10%)
  other arithmetic  7.2 us (5%)
  local copies, waits for them, and re-layouts  2.63 us (2%)
    pallas_call x1, Pallas kernels, pair_coefficients(): pl.pallas_call(functools.partial(pair_kernel, side, planes, norm, early,...  35.8 us
    pallas_call x2, Pallas kernels, coulomb_partial(): pl.pallas_call(functools.partial(coulomb_kernel, freq, shares, scale, own...  35.1 us
    ppermute x7, waiting for transfers between devices, shards(): same[shift ^ 1 << bit] = lax.ppermute(same[shift], 'row', hop)  18.3 us
    all_to_all x1, blocking collectives, shards(): lax.all_to_all(partial, axes, split_axis=0, concat_axis=0, tiled=True)  16.3 us
    pallas_call x1, Pallas kernels, plane_lines(): pl.pallas_call(functools.partial(plane_kernel, side, planes), out_shape=j...  14.9 us
    ppermute x7, starting transfers between devices, shards(): same[shift ^ 1 << bit] = lax.ppermute(same[shift], 'row', hop)  11.1 us
    ppermute x1, waiting for transfers between devices, shards(): recv = lax.ppermute(send, 'col', swap)  6.75 us
    all_to_all x1, starting transfers between devices, shards(): lax.all_to_all(partial, axes, split_axis=0, concat_axis=0, tiled=True)  5.52 us
  transfers between devices with their start and end apart: 18, of which 8 were waited for; matrix products, arithmetic and copies ran while one was open for 4% of the time, Pallas kernels for 21%

profile of v4, /device:TPU:0, one launch (start us, length us, event | category | flops | bytes accessed | tf_op | source)
XLA Modules:
  0.0 157.7 jit_solution(5782122390437381688)
XLA Ops:
  0.0 1.0 copy.11
  1.0 4.1 %collective-permute-start.7 = (f32[2,32,1024]{2,1,0:T(8,128)S(1)}, f32[2,32,1024]{2,1,0:T(8,128)}, u32[]{:S(2)}, u32[]{:S(2)}) collective-permute-start(f32[2,32,1024]{2,1,0:T(8,128)S(1)} %bitcast.13), channel_id=1, source_target_pairs={{0,8},{2,10},{4,12},{6,14},{8,0},{10,2},{12,4},{14,6},{1,9},{3,11}... | collective-permute-start | bytes 786440 | tf_op jit(solution)/shard_map/ppermute | solution.py:460
  5.2 0.0 collective-permute-start.3
  5.2 1.6 collective-permute-start.1
  6.8 1.5 collective-permute-start
  8.3 0.9 fusion.8
  9.2 0.8 compare_select_fusion
  10.0 0.8 constant_dynamic-slice_fusion
  10.7 0.7 constant_dynamic-slice_fusion.1
  11.5 0.6 maximum_bitcast_fusion.signs
  12.1 5.2 %collective-permute-done.7.refs_1_ = f32[2,32,1024]{2,1,0:T(8,128)} collective-permute-done((f32[2,32,1024]{2,1,0:T(8,128)S(1)}, f32[2,32,1024]{2,1,0:T(8,128)}, u32[]{:S(2)}, u32[]{:S(2)}) %collective-permute-start.7) | collective-permute-done | bytes 262176 | tf_op jit(solution)/shard_map/ppermute | solution.py:460
  17.3 0.6 collective-permute-start.9
  17.9 0.5 collective-permute-done.1.refs_2_
  18.4 1.6 collective-permute-start.2
  19.9 0.6 pad_add_fusion.cells
  20.6 0.5 collective-permute-start.8
  21.0 0.0 collective-permute-start.5
  21.0 0.0 collective-permute-done.refs_1_
  21.0 0.5 collective-permute-start.4
  21.5 3.5 %collective-permute-done.9.refs_3_ = f32[2,32,1024]{2,1,0:T(8,128)} collective-permute-done((f32[2,32,1024]{2,1,0:T(8,128)}, f32[2,32,1024]{2,1,0:T(8,128)}, u32[]{:S(2)}, u32[]{:S(2)}) %collective-permute-start.9) | collective-permute-done | bytes 262176 | tf_op jit(solution)/shard_map/ppermute | solution.py:460
  25.0 1.3 collective-permute-start.10
  26.4 1.2 collective-permute-done.2.refs_3_
  27.5 0.0 collective-permute-start.6
  27.5 0.6 pad_add_fusion.1.info
  28.1 0.1 eq.25
  28.2 0.8 compare_convert_fusion.refs_8_.refs_9_
  29.0 4.3 %collective-permute-done.8.refs_2_ = f32[2,32,1024]{2,1,0:T(8,128)} collective-permute-done((f32[2,32,1024]{2,1,0:T(8,128)}, f32[2,32,1024]{2,1,0:T(8,128)}, u32[]{:S(2)}, u32[]{:S(2)}) %collective-permute-start.8) | collective-permute-done | bytes 262176 | tf_op jit(solution)/shard_map/ppermute | solution.py:460
  33.3 0.0 collective-permute-start.11
  33.3 0.0 collective-permute-done.5.refs_6_
  33.3 0.6 collective-permute-start.13
  33.8 0.0 collective-permute-done.4.refs_5_
  33.8 0.1 collective-permute-start.12
  34.0 0.0 copy-done.5
  34.0 3.6 %collective-permute-done.10.refs_4_ = f32[2,32,1024]{2,1,0:T(8,128)} collective-permute-done((f32[2,32,1024]{2,1,0:T(8,128)}, f32[2,32,1024]{2,1,0:T(8,128)}, u32[]{:S(2)}, u32[]{:S(2)}) %collective-permute-start.10) | collective-permute-done | bytes 262176 | tf_op jit(solution)/shard_map/ppermute | solution.py:460
  37.6 0.0 collective-permute-start.14
  37.6 14.9 %plane_lines.1.refs_0_ = bf16[8,136,16,256]{3,2,1,0:T(8,128)(2,1)} custom-call(s32[2]{0:T(128)} %pad_add_fusion.1.info, f32[2,32,1024]{2,1,0:T(8,128)} %bitcast.17, f32[2,32,1024]{2,1,0:T(8,128)} %copy-done.3, f32[2,32,1024]{2,1,0:T(8,128)} %copy-done.2, f32[2,32,1024]{2,1,0:T(8,128)} %copy-done.4, f32[2,32,1024]{2,1,0:T(8,128)} %copy-done.1, ...), custom_call_target="tpu_custom_call" | custom-call | flops 4800000000 | bytes 6000000 | tf_op jit(solution)/shard_map/plane_lines/pallas_call | solution.py:143
  52.5 35.8 %pair_coefficients.1 = (bf16[384,5120]{1,0:T(8,128)(2,1)}, bf16[384,4096]{1,0:T(8,128)(2,1)}) custom-call(s32[2]{0:T(128)} %pad_add_fusion.1.info, s32[9216]{0:T(1024)} %pad_add_fusion.cells, f32[72,128]{1,0:T(8,128)} %maximum_bitcast_fusion.signs, bf16[8,136,16,256]{3,2,1,0:T(8,128)(2,1)} %plane_lines.1.refs_0_, ...), custom_call_target="tpu_custom_call" | custom-call | flops 20000000000 | bytes 25000000 | tf_op jit(solution)/shard_map/pair_coefficients/pallas_call | solution.py:273
  88.3 0.6 collective-permute-start.15
  88.9 6.8 %collective-permute-done.15.recv = bf16[384,5120]{1,0:T(8,128)(2,1)} collective-permute-done((bf16[384,5120]{1,0:T(8,128)(2,1)}, bf16[384,5120]{1,0:T(8,128)(2,1)}, u32[]{:S(2)}, u32[]{:S(2)}) %collective-permute-start.15) | collective-permute-done | bytes 3932192 | tf_op jit(solution)/shard_map/ppermute | solution.py:493
  95.6 17.5 %coulomb_partial.2.refs_0_ = bf16[16,2,24,384]{3,2,1,0:T(8,128)(2,1)} custom-call(s32[2]{0:T(128)} %pad_add_fusion.1.info, bf16[384,4096]{1,0:T(8,128)(2,1)} %get-tuple-element.17.keep, bf16[384,5120]{1,0:T(8,128)(2,1)} %get-tuple-element.18.send, bf16[384,5120]{1,0:T(8,128)(2,1)} %collective-permute-done.15.recv, bf16[2,2,1024,4096]{3,2,1,0:T(8,128)(2,1)} %w.3), custom_call_target="tpu_custom_call" | custom-call | flops 14000000000 | bytes 25000000 | tf_op jit(solution)/shard_map/coulomb_partial/pallas_call | solution.py:414
  113.1 5.5 %all-to-all-start = ((bf16[16,2,24,384]{3,2,1,0:T(8,128)(2,1)}), bf16[16,2,24,384]{3,2,1,0:T(8,128)(2,1)}, u32[]{:S(2)}, u32[]{:S(2)}) async-start(bf16[16,2,24,384]{3,2,1,0:T(8,128)(2,1)} %coulomb_partial.2.refs_0_), calls=%async_computation | async-start | bytes 1179648 | tf_op jit(solution)/shard_map/all_to_all | solution.py:508
  118.7 17.6 %coulomb_partial.3 = bf16[16,2,24,384]{3,2,1,0:T(8,128)(2,1)} custom-call(s32[2]{0:T(128)} %pad_add_fusion.1.info, bf16[384,4096]{1,0:T(8,128)(2,1)} %get-tuple-element.17.keep, bf16[384,5120]{1,0:T(8,128)(2,1)} %get-tuple-element.18.send, bf16[384,5120]{1,0:T(8,128)(2,1)} %collective-permute-done.15.recv, bf16[2,2,1024,4096]{3,2,1,0:T(8,128)(2,1)} %w.3, ...), custom_call_target="tpu_custom_call" | custom-call | flops 14000000000 | bytes 25000000 | tf_op jit(solution)/shard_map/coulomb_partial/pallas_call | solution.py:414
  136.2 0.4 collective-permute-start.16
  136.7 1.9 %collective-permute-done.16 = bf16[16,2,24,384]{3,2,1,0:T(8,128)(2,1)S(1)} collective-permute-done((bf16[16,2,24,384]{3,2,1,0:T(8,128)(2,1)}, bf16[16,2,24,384]{3,2,1,0:T(8,128)(2,1)S(1)}, u32[]{:S(2)}, u32[]{:S(2)}) %collective-permute-start.16) | collective-permute-done | bytes 589856 | tf_op jit(solution)/shard_map/ppermute | solution.py:504
  138.5 1.0 add_convert_fusion
  139.6 1.2 convert_reduce_fusion
  140.7 16.3 %all_to_all.10 = bf16[8,2,24,384]{3,2,1,0:T(8,128)(2,1)S(1)} all-to-all(bf16[8,2,24,384]{3,2,1,0:T(8,128)(2,1)S(1)} %add_convert_fusion), channel_id=1, replica_groups=mesh['kpt'=2,'row'=8,'col'=2] {'row'}, dimensions={0} | all-to-all | bytes 589824 | tf_op jit(solution)/shard_map/all_to_all | solution.py:508
  157.1 0.7 pad_maximum_fusion
  (27 shorter events, 0.1 us)
Async XLA Ops:
  1.0 5.7 %copy-start = (f32[32,2,1024]{2,0,1:T(8,128)}, f32[32,2,1024]{2,0,1:T(8,128)S(1)}, u32[]{:S(2)}) copy-start(f32[32,2,1024]{2,0,1:T(8,128)S(1)} %copy.11) | copy-start | bytes 786436
  1.0 16.3 %collective-permute-start.7 = (f32[2,32,1024]{2,1,0:T(8,128)S(1)}, f32[2,32,1024]{2,1,0:T(8,128)}, u32[]{:S(2)}, u32[]{:S(2)}) collective-permute-start(f32[2,32,1024]{2,1,0:T(8,128)S(1)} %bitcast.13), channel_id=1, source_target_pairs={{0,8},{2,10},{4,12},{6,14},{8,0},{10,2},{12,4},{14,6},{1,9},{3,11}... | collective-permute-start | bytes 786440 | tf_op jit(solution)/shard_map/ppermute | solution.py:460
  5.2 15.8 %collective-permute-start.3 = (f32[2,32,1024]{2,1,0:T(8,128)S(1)}, f32[2,32,1024]{2,1,0:T(8,128)S(1)}, u32[]{:S(2)}, u32[]{:S(2)}) collective-permute-start(f32[2,32,1024]{2,1,0:T(8,128)S(1)} %bitcast.14), channel_id=1, source_target_pairs={{0,1},{1,0},{2,3},{3,2},{4,5},{5,4},{6,7},{7,6},{8,9},{9,8},{10,11... | collective-permute-start | bytes 786440 | tf_op jit(solution)/shard_map/ppermute | solution.py:463
  5.2 13.2 %collective-permute-start.1 = (f32[2,32,1024]{2,1,0:T(8,128)S(1)}, f32[2,32,1024]{2,1,0:T(8,128)S(1)}, u32[]{:S(2)}, u32[]{:S(2)}) collective-permute-start(f32[2,32,1024]{2,1,0:T(8,128)S(1)} %bitcast.15), channel_id=1, source_target_pairs={{0,4},{2,6},{4,0},{6,2},{8,12},{10,14},{12,8},{14,10},{1,5},{3,7},... | collective-permute-start | bytes 786440 | tf_op jit(solution)/shard_map/ppermute | solution.py:460
  6.8 14.3 %collective-permute-start = (f32[2,32,1024]{2,1,0:T(8,128)S(1)}, f32[2,32,1024]{2,1,0:T(8,128)S(1)}, u32[]{:S(2)}, u32[]{:S(2)}) collective-permute-start(f32[2,32,1024]{2,1,0:T(8,128)S(1)} %bitcast.16), channel_id=1, source_target_pairs={{0,2},{2,0},{4,6},{6,4},{8,10},{10,8},{12,14},{14,12},{1,3},{3,1},... | collective-permute-start | bytes 786440 | tf_op jit(solution)/shard_map/ppermute | solution.py:460
  17.3 7.7 %collective-permute-start.9 = (f32[2,32,1024]{2,1,0:T(8,128)}, f32[2,32,1024]{2,1,0:T(8,128)}, u32[]{:S(2)}, u32[]{:S(2)}) collective-permute-start(f32[2,32,1024]{2,1,0:T(8,128)} %collective-permute-done.7.refs_1_), channel_id=1, source_target_pairs={{0,4},{2,6},{4,0},{6,2},{8,12},{10,14},{12,8},{14,10},{1,5},{3,7},... | collective-permute-start | bytes 786440 | tf_op jit(solution)/shard_map/ppermute | solution.py:460
  18.4 14.9 %copy-start.2 = (f32[2,32,1024]{2,1,0:T(8,128)}, f32[2,32,1024]{2,1,0:T(8,128)S(1)}, u32[]{:S(2)}) copy-start(f32[2,32,1024]{2,1,0:T(8,128)S(1)} %collective-permute-done.1.refs_2_) | copy-start | bytes 786436
  18.4 9.2 %collective-permute-start.2 = (f32[2,32,1024]{2,1,0:T(8,128)S(1)}, f32[2,32,1024]{2,1,0:T(8,128)S(1)}, u32[]{:S(2)}, u32[]{:S(2)}) collective-permute-start(f32[2,32,1024]{2,1,0:T(8,128)S(1)} %collective-permute-done.1.refs_2_), channel_id=1, source_target_pairs={{0,2},{2,0},{4,6},{6,4},{8,10},{10,8},{12,14},{14,12},{1,3},{3,1},... | collective-permute-start | bytes 786440 | tf_op jit(solution)/shard_map/ppermute | solution.py:460
  20.6 12.7 %collective-permute-start.8 = (f32[2,32,1024]{2,1,0:T(8,128)}, f32[2,32,1024]{2,1,0:T(8,128)}, u32[]{:S(2)}, u32[]{:S(2)}) collective-permute-start(f32[2,32,1024]{2,1,0:T(8,128)} %collective-permute-done.7.refs_1_), channel_id=1, source_target_pairs={{0,2},{2,0},{4,6},{6,4},{8,10},{10,8},{12,14},{14,12},{1,3},{3,1},... | collective-permute-start | bytes 786440 | tf_op jit(solution)/shard_map/ppermute | solution.py:460
  21.0 8.0 %copy-start.1 = (f32[2,32,1024]{2,1,0:T(8,128)}, f32[2,32,1024]{2,1,0:T(8,128)S(1)}, u32[]{:S(2)}) copy-start(f32[2,32,1024]{2,1,0:T(8,128)S(1)} %collective-permute-done.3.refs_4_) | copy-start | bytes 786436
  21.0 12.3 %collective-permute-start.5 = (f32[2,32,1024]{2,1,0:T(8,128)S(1)}, f32[2,32,1024]{2,1,0:T(8,128)S(1)}, u32[]{:S(2)}, u32[]{:S(2)}) collective-permute-start(f32[2,32,1024]{2,1,0:T(8,128)S(1)} %collective-permute-done.1.refs_2_), channel_id=1, source_target_pairs={{0,1},{1,0},{2,3},{3,2},{4,5},{5,4},{6,7},{7,6},{8,9},{9,8},{10,11... | collective-permute-start | bytes 786440 | tf_op jit(solution)/shard_map/ppermute | solution.py:463
  21.0 12.2 %copy-start.3 = (f32[2,32,1024]{2,1,0:T(8,128)}, f32[2,32,1024]{2,1,0:T(8,128)S(1)}, u32[]{:S(2)}) copy-start(f32[2,32,1024]{2,1,0:T(8,128)S(1)} %collective-permute-done.refs_1_) | copy-start | bytes 786436
  21.0 12.8 %collective-permute-start.4 = (f32[2,32,1024]{2,1,0:T(8,128)S(1)}, f32[2,32,1024]{2,1,0:T(8,128)S(1)}, u32[]{:S(2)}, u32[]{:S(2)}) collective-permute-start(f32[2,32,1024]{2,1,0:T(8,128)S(1)} %collective-permute-done.refs_1_), channel_id=1, source_target_pairs={{0,1},{1,0},{2,3},{3,2},{4,5},{5,4},{6,7},{7,6},{8,9},{9,8},{10,11... | collective-permute-start | bytes 786440 | tf_op jit(solution)/shard_map/ppermute | solution.py:463
  25.0 12.5 %collective-permute-start.10 = (f32[2,32,1024]{2,1,0:T(8,128)}, f32[2,32,1024]{2,1,0:T(8,128)}, u32[]{:S(2)}, u32[]{:S(2)}) collective-permute-start(f32[2,32,1024]{2,1,0:T(8,128)} %collective-permute-done.9.refs_3_), channel_id=1, source_target_pairs={{0,2},{2,0},{4,6},{6,4},{8,10},{10,8},{12,14},{14,12},{1,3},{3,1},... | collective-permute-start | bytes 786440 | tf_op jit(solution)/shard_map/ppermute | solution.py:460
  27.5 6.3 %copy-start.4 = (f32[2,32,1024]{2,1,0:T(8,128)}, f32[2,32,1024]{2,1,0:T(8,128)S(1)}, u32[]{:S(2)}) copy-start(f32[2,32,1024]{2,1,0:T(8,128)S(1)} %collective-permute-done.2.refs_3_) | copy-start | bytes 786436
  27.5 10.0 %collective-permute-start.6 = (f32[2,32,1024]{2,1,0:T(8,128)S(1)}, f32[2,32,1024]{2,1,0:T(8,128)}, u32[]{:S(2)}, u32[]{:S(2)}) collective-permute-start(f32[2,32,1024]{2,1,0:T(8,128)S(1)} %collective-permute-done.2.refs_3_), channel_id=1, source_target_pairs={{0,1},{1,0},{2,3},{3,2},{4,5},{5,4},{6,7},{7,6},{8,9},{9,8},{10,11... | collective-permute-start | bytes 786440 | tf_op jit(solution)/shard_map/ppermute | solution.py:463
  33.3 19.2 %collective-permute-start.11 = (f32[2,32,1024]{2,1,0:T(8,128)}, f32[2,32,1024]{2,1,0:T(8,128)}, u32[]{:S(2)}, u32[]{:S(2)}) collective-permute-start(f32[2,32,1024]{2,1,0:T(8,128)} %collective-permute-done.7.refs_1_), channel_id=1, source_target_pairs={{0,1},{1,0},{2,3},{3,2},{4,5},{5,4},{6,7},{7,6},{8,9},{9,8},{10,11... | collective-permute-start | bytes 786440 | tf_op jit(solution)/shard_map/ppermute | solution.py:463
  33.3 0.7 copy-start.5
  33.3 19.2 %collective-permute-start.13 = (f32[2,32,1024]{2,1,0:T(8,128)}, f32[2,32,1024]{2,1,0:T(8,128)}, u32[]{:S(2)}, u32[]{:S(2)}) collective-permute-start(f32[2,32,1024]{2,1,0:T(8,128)} %collective-permute-done.9.refs_3_), channel_id=1, source_target_pairs={{0,1},{1,0},{2,3},{3,2},{4,5},{5,4},{6,7},{7,6},{8,9},{9,8},{10,11... | collective-permute-start | bytes 786440 | tf_op jit(solution)/shard_map/ppermute | solution.py:463
  33.8 3.7 %copy-start.6 = (f32[2,32,1024]{2,1,0:T(8,128)}, f32[2,32,1024]{2,1,0:T(8,128)S(1)}, u32[]{:S(2)}) copy-start(f32[2,32,1024]{2,1,0:T(8,128)S(1)} %collective-permute-done.4.refs_5_) | copy-start | bytes 786436
  33.8 18.6 %collective-permute-start.12 = (f32[2,32,1024]{2,1,0:T(8,128)}, f32[2,32,1024]{2,1,0:T(8,128)}, u32[]{:S(2)}, u32[]{:S(2)}) collective-permute-start(f32[2,32,1024]{2,1,0:T(8,128)} %collective-permute-done.8.refs_2_), channel_id=1, source_target_pairs={{0,1},{1,0},{2,3},{3,2},{4,5},{5,4},{6,7},{7,6},{8,9},{9,8},{10,11... | collective-permute-start | bytes 786440 | tf_op jit(solution)/shard_map/ppermute | solution.py:463
  37.6 14.9 %collective-permute-start.14 = (f32[2,32,1024]{2,1,0:T(8,128)}, f32[2,32,1024]{2,1,0:T(8,128)}, u32[]{:S(2)}, u32[]{:S(2)}) collective-permute-start(f32[2,32,1024]{2,1,0:T(8,128)} %collective-permute-done.10.refs_4_), channel_id=1, source_target_pairs={{0,1},{1,0},{2,3},{3,2},{4,5},{5,4},{6,7},{7,6},{8,9},{9,8},{10,11... | collective-permute-start | bytes 786440 | tf_op jit(solution)/shard_map/ppermute | solution.py:463
  88.3 7.3 %collective-permute-start.15 = (bf16[384,5120]{1,0:T(8,128)(2,1)}, bf16[384,5120]{1,0:T(8,128)(2,1)}, u32[]{:S(2)}, u32[]{:S(2)}) collective-permute-start(bf16[384,5120]{1,0:T(8,128)(2,1)} %get-tuple-element.18.send), channel_id=1, source_target_pairs={{0,1},{1,0},{2,3},{3,2},{4,5},{5,4},{6,7},{7,6},{8,9},{9,8},{10,11... | collective-permute-start | bytes 11796488 | tf_op jit(solution)/shard_map/ppermute | solution.py:493
  113.1 26.4 %all-to-all-start = ((bf16[16,2,24,384]{3,2,1,0:T(8,128)(2,1)}), bf16[16,2,24,384]{3,2,1,0:T(8,128)(2,1)}, u32[]{:S(2)}, u32[]{:S(2)}) async-start(bf16[16,2,24,384]{3,2,1,0:T(8,128)(2,1)} %coulomb_partial.2.refs_0_), calls=%async_computation | async-start | bytes 1179648 | tf_op jit(solution)/shard_map/all_to_all | solution.py:508
  136.2 2.3 %collective-permute-start.16 = (bf16[16,2,24,384]{3,2,1,0:T(8,128)(2,1)}, bf16[16,2,24,384]{3,2,1,0:T(8,128)(2,1)S(1)}, u32[]{:S(2)}, u32[]{:S(2)}) collective-permute-start(bf16[16,2,24,384]{3,2,1,0:T(8,128)(2,1)} %coulomb_partial.3), channel_id=1, source_target_pairs={{0,1},{1,0},{2,3},{3,2},{4,5},{5,4},{6,7},{7,6},{8,9},{9,8},{10,11... | collective-permute-start | bytes 1769480 | tf_op jit(solution)/shard_map/ppermute | solution.py:504
